TPU v7x, 256 devices: a whole 4x4x8 slice. The times are simulated.
256 devices in a mesh: gx: 8 (over y, core), gz: 8 (over z), gy: 4 (over x).
Axes of the slice: x: 4, y: 4, z: 8, core: 2. Of those that a mesh axis runs over, the one named last changes fastest.
Arguments:
- logits: float32 [256, 1048576], P('gy', ('gx', 'gz')), may hold values from -60 to 250
Outputs:
- token_potential: float32 [1048576], P(('gx', 'gz'))
- expert_potential: float32 [256], P('gy')
All inputs are finite; a program needn't handle non-finite values.
Results may differ from a plain program's by a relative error of at most 0.0001.
Values sent between devices are 32-bit elements; how exact they have to be, the bound alone decides.
No kernel may reach another device: no remote copies, remote signals or barrier semaphores. Data moves between devices by JAX's collectives and lax.ppermute only.
A program may use at most 64 MiB of HBM per device.

v0:
```python
import jax
import jax.numpy as jnp
from jax import lax
from jax.sharding import PartitionSpec as P

ITERS = 3


def from_everyone(array, axis):
    copies = jnp.broadcast_to(array, (lax.axis_size(axis), *array.shape))
    return lax.all_to_all(copies, axis, split_axis=0, concat_axis=0, tiled=True)


def collected_together(array, axis):
    leaves = jax.tree.leaves(array)
    turns = sorted(range(len(leaves)), key=lambda k: -leaves[k].size)
    width = (1, *leaves[turns[0]].shape)[-1]
    lines = [
        jnp.pad(leaves[k].reshape(-1), (0, -leaves[k].size % width)).reshape(-1, width)
        for k in turns
    ]
    both, at, found = (from_everyone(jnp.concatenate(lines), axis), 0, {})
    for k, line in zip(turns, lines):
        slab = both[:, at : at + len(line)].reshape(len(both), -1)
        found[k] = slab[:, : leaves[k].size].reshape(-1, *leaves[k].shape)
        at += len(line)
    numbers = iter(range(len(leaves)))
    return jax.tree.map(lambda _: found[next(numbers)], array)


def folded_in_pairs(pieces, combine):
    while len(jax.tree.leaves(pieces)[0]) > 1:
        pieces = jax.vmap(combine)(
            *(jax.tree.map(lambda part: part[side::2], pieces) for side in (0, 1))
        )
    return jax.tree.map(lambda part: part[0], pieces)


def combined_all(array, axis, combine):
    pieces = collected_together(array, axis)
    return folded_in_pairs(pieces, combine)


def joined_all(array, axis, combine):
    pieces = jax.tree.map(lambda part: from_everyone(part, axis), array)
    return folded_in_pairs(pieces, combine)


def pair_join(first, second):
    top = jnp.maximum(first[0], second[0])
    return (top, first[1] * jnp.exp(first[0] - top) + second[1] * jnp.exp(second[0] - top))


def per_device(logits):
    local_experts = logits.shape[0]
    local_tokens = logits.shape[1]
    all_tokens = local_tokens * lax.axis_size("gx") * lax.axis_size("gz")
    all_experts = local_experts * lax.axis_size("gy")
    log_cap = jnp.log(jnp.float32(all_tokens) / jnp.float32(all_experts))
    token_potential = jnp.zeros((local_tokens,), jnp.float32)
    expert_potential = jnp.zeros((local_experts,), jnp.float32)
    for step in range(ITERS):
        shifted = logits + token_potential[None, :]
        top = jnp.max(shifted, axis=1)
        local_total = jnp.sum(jnp.exp(shifted - top[:, None]), axis=1)
        top, total = combined_all((top, local_total), ("gx", "gz"), pair_join)
        expert_potential = log_cap - (top + jnp.log(total))
        raised = logits + expert_potential[:, None]
        peak = jnp.max(raised, axis=0)
        local_summed = jnp.sum(jnp.exp(raised - peak[None, :]), axis=0)
        peak, summed = joined_all((peak, local_summed), "gy", pair_join)
        token_potential = -(peak + jnp.log(summed))
    return (token_potential, expert_potential)


def solution(mesh):
    in_specs = (P("gy", ("gx", "gz")),)
    out_specs = (P(("gx", "gz")), P("gy"))
    return jax.shard_map(
        per_device, mesh=mesh, in_specs=in_specs, out_specs=out_specs, check_vma=False
    )
```

profile of v0, /device:TPU:8, one launch (start us, length us, event | category | flops | bytes accessed | tf_op | source)
XLA Modules:
  0.0 149.5 jit_solution(11057812459159432661)
XLA Ops:
  0.6 2.5 %reduce_max.54 = f32[64]{0:T(128)S(1)} reduce(f32[64,16384]{1,0:T(8,128)} %param.1, f32[]{:T(128)} %constant.0.clone.1), dimensions={1}, to_apply=%region_0.0 | reduce | flops 1048512 | bytes 4194564 | tf_op jit(solution)/shard_map/reduce_max | solution.py:64
  3.1 2.9 %exponential_reduce_fusion.5 = f32[64]{0:T(128)S(1)} fusion(f32[64,16384]{1,0:T(8,128)} %param.1, f32[64]{0:T(128)S(1)} %reduce_max.54), kind=kLoop, calls=%fused_computation.5 | loop fusion | flops 2097088 | bytes 4194816 | tf_op jit(solution)/shard_map/reduce_sum | solution.py:65
  6.1 0.1 reshape.130
  6.2 20.6 %all_to_all.69 = f32[64,1,128]{2,1,0:T(1,128)S(1)} all-to-all(f32[64,1,128]{2,1,0:T(1,128)S(1)} %reshape.130), channel_id=1, replica_groups=mesh['gx'=8,'gz'=8,'gy'=4] {'gx','gz'}, dimensions={0} | all-to-all | bytes 65536 | tf_op jit(solution)/shard_map/all_to_all | solution.py:11
  26.8 0.5 broadcast.47
  27.3 0.7 reduce
  28.7 2.7 %add_reduce_fusion.4 = f32[16384]{0:T(1024)S(1)} fusion(f32[64,16384]{1,0:T(8,128)} %param.1, f32[64]{0:T(128)S(1)} %subtract_bitcast_fusion.2), kind=kLoop, calls=%fused_computation.10 | loop fusion | flops 2080768 | bytes 4260096 | tf_op jit(solution)/shard_map/reduce_max | solution.py:69
  31.4 0.8 broadcast_in_dim.19
  32.2 4.3 %all-to-all-start.1 = ((f32[4,1,16384]{2,1,0:T(1,128)}), f32[4,1,16384]{2,1,0:T(1,128)S(1)}, u32[]{:S(2)}, u32[]{:S(2)}) async-start(f32[4,1,16384]{2,1,0:T(1,128)} %broadcast_in_dim.19), calls=%async_computation.1 | async-start | bytes 524288 | tf_op jit(solution)/shard_map/all_to_all | solution.py:11
  36.5 3.0 %exponential_reduce_fusion.4 = f32[16384]{0:T(1024)S(1)} fusion(f32[64,16384]{1,0:T(8,128)} %param.1, f32[16384]{0:T(1024)S(1)} %add_reduce_fusion.4, f32[64]{0:T(128)S(1)} %subtract_bitcast_fusion.2), kind=kLoop, calls=%fused_computation.4 | loop fusion | flops 3129344 | bytes 4325632 | tf_op jit(solution)/shard_map/reduce_sum | solution.py:70
  39.5 3.6 %all-to-all-done.1 = f32[4,1,16384]{2,1,0:T(1,128)S(1)} async-done(((f32[4,1,16384]{2,1,0:T(1,128)}), f32[4,1,16384]{2,1,0:T(1,128)S(1)}, u32[]{:S(2)}, u32[]{:S(2)}) %all-to-all-start.1) | async-done | bytes 262176 | tf_op jit(solution)/shard_map/all_to_all | solution.py:11
  43.2 0.8 broadcast_in_dim.40
  44.0 3.4 %all-to-all-start.2 = ((f32[4,1,16384]{2,1,0:T(1,128)}), f32[4,1,16384]{2,1,0:T(1,128)S(1)}, u32[]{:S(2)}, u32[]{:S(2)}) async-start(f32[4,1,16384]{2,1,0:T(1,128)} %broadcast_in_dim.40), calls=%async_computation.2 | async-start | bytes 524288 | tf_op jit(solution)/shard_map/all_to_all | solution.py:11
  47.4 0.2 copy.35
  47.6 1.0 slice.357
  48.6 1.0 slice.356
  49.6 4.4 %all-to-all-done.2 = f32[4,1,16384]{2,1,0:T(1,128)S(1)} async-done(((f32[4,1,16384]{2,1,0:T(1,128)}), f32[4,1,16384]{2,1,0:T(1,128)S(1)}, u32[]{:S(2)}, u32[]{:S(2)}) %all-to-all-start.2) | async-done | bytes 262176 | tf_op jit(solution)/shard_map/all_to_all | solution.py:11
  54.0 0.2 copy.34
  54.2 1.0 slice.361
  55.2 1.0 slice.360
  56.3 0.2 multiply_add_fusion.2
  56.4 0.3 add_negate_fusion.2
  56.8 2.9 %add_reduce_fusion.3 = f32[64]{0:T(128)S(1)} fusion(f32[64,16384]{1,0:T(8,128)} %param.1, f32[16384]{0:T(1024)S(1)} %bitcast.61), kind=kLoop, calls=%fused_computation.9 | loop fusion | flops 2097088 | bytes 4260096 | tf_op jit(solution)/shard_map/reduce_max | solution.py:64
  59.7 0.9 exponential_reduce_fusion.3
  60.7 0.1 reshape.132
  60.8 13.4 %all_to_all.70 = f32[64,1,128]{2,1,0:T(1,128)S(1)} all-to-all(f32[64,1,128]{2,1,0:T(1,128)S(1)} %reshape.132), channel_id=1, replica_groups=mesh['gx'=8,'gz'=8,'gy'=4] {'gx','gz'}, dimensions={0} | all-to-all | bytes 65536 | tf_op jit(solution)/shard_map/all_to_all | solution.py:11
  74.2 0.7 reduce.1
  75.6 2.7 %add_reduce_fusion.2 = f32[16384]{0:T(1024)S(1)} fusion(f32[64,16384]{1,0:T(8,128)} %param.1, f32[64]{0:T(128)S(1)} %subtract_bitcast_fusion.1), kind=kLoop, calls=%fused_computation.8 | loop fusion | flops 2080768 | bytes 4260096 | tf_op jit(solution)/shard_map/reduce_max | solution.py:69
  78.2 0.8 broadcast_in_dim.42
  79.1 3.4 %all-to-all-start.4 = ((f32[4,1,16384]{2,1,0:T(1,128)}), f32[4,1,16384]{2,1,0:T(1,128)S(1)}, u32[]{:S(2)}, u32[]{:S(2)}) async-start(f32[4,1,16384]{2,1,0:T(1,128)} %broadcast_in_dim.42), calls=%async_computation.4 | async-start | bytes 524288 | tf_op jit(solution)/shard_map/all_to_all | solution.py:11
  82.5 3.0 %exponential_reduce_fusion.2 = f32[16384]{0:T(1024)S(1)} fusion(f32[64,16384]{1,0:T(8,128)} %param.1, f32[16384]{0:T(1024)S(1)} %add_reduce_fusion.2, f32[64]{0:T(128)S(1)} %subtract_bitcast_fusion.1), kind=kLoop, calls=%fused_computation.2 | loop fusion | flops 3129344 | bytes 4325632 | tf_op jit(solution)/shard_map/reduce_sum | solution.py:70
  85.5 3.7 %all-to-all-done.4 = f32[4,1,16384]{2,1,0:T(1,128)S(1)} async-done(((f32[4,1,16384]{2,1,0:T(1,128)}), f32[4,1,16384]{2,1,0:T(1,128)S(1)}, u32[]{:S(2)}, u32[]{:S(2)}) %all-to-all-start.4) | async-done | bytes 262176 | tf_op jit(solution)/shard_map/all_to_all | solution.py:11
  89.2 0.8 broadcast_in_dim.43
  90.0 3.6 %all-to-all-start.5 = ((f32[4,1,16384]{2,1,0:T(1,128)}), f32[4,1,16384]{2,1,0:T(1,128)S(1)}, u32[]{:S(2)}, u32[]{:S(2)}) async-start(f32[4,1,16384]{2,1,0:T(1,128)} %broadcast_in_dim.43), calls=%async_computation.5 | async-start | bytes 524288 | tf_op jit(solution)/shard_map/all_to_all | solution.py:11
  93.6 0.2 copy.33
  93.8 1.0 slice.391
  94.8 1.0 slice.390
  95.8 4.3 %all-to-all-done.5 = f32[4,1,16384]{2,1,0:T(1,128)S(1)} async-done(((f32[4,1,16384]{2,1,0:T(1,128)}), f32[4,1,16384]{2,1,0:T(1,128)S(1)}, u32[]{:S(2)}, u32[]{:S(2)}) %all-to-all-start.5) | async-done | bytes 262176 | tf_op jit(solution)/shard_map/all_to_all | solution.py:11
  100.1 0.2 copy.32
  100.3 1.0 slice.395
  101.3 1.0 slice.394
  102.3 0.2 multiply_add_fusion.1
  102.5 0.3 add_negate_fusion.1
  102.8 2.9 %add_reduce_fusion.1 = f32[64]{0:T(128)S(1)} fusion(f32[64,16384]{1,0:T(8,128)} %param.1, f32[16384]{0:T(1024)S(1)} %bitcast.63), kind=kLoop, calls=%fused_computation.7 | loop fusion | flops 2097088 | bytes 4260096 | tf_op jit(solution)/shard_map/reduce_max | solution.py:64
  105.8 0.9 exponential_reduce_fusion.1
  106.7 0.1 reshape.134
  106.8 13.4 %all_to_all.71 = f32[64,1,128]{2,1,0:T(1,128)S(1)} all-to-all(f32[64,1,128]{2,1,0:T(1,128)S(1)} %reshape.134), channel_id=1, replica_groups=mesh['gx'=8,'gz'=8,'gy'=4] {'gx','gz'}, dimensions={0} | all-to-all | bytes 65536 | tf_op jit(solution)/shard_map/all_to_all | solution.py:11
  120.3 0.7 reduce.2
  121.6 2.6 %add_reduce_fusion = f32[16384]{0:T(1024)S(1)} fusion(f32[64,16384]{1,0:T(8,128)} %param.1, f32[64]{0:T(128)S(1)} %subtract_bitcast_fusion), kind=kLoop, calls=%fused_computation.6 | loop fusion | flops 2080768 | bytes 4260096 | tf_op jit(solution)/shard_map/reduce_max | solution.py:69
  124.3 0.8 broadcast_in_dim.45
  125.1 3.4 %all-to-all-start.7 = ((f32[4,1,16384]{2,1,0:T(1,128)}), f32[4,1,16384]{2,1,0:T(1,128)S(1)}, u32[]{:S(2)}, u32[]{:S(2)}) async-start(f32[4,1,16384]{2,1,0:T(1,128)} %broadcast_in_dim.45), calls=%async_computation.7 | async-start | bytes 524288 | tf_op jit(solution)/shard_map/all_to_all | solution.py:11
  128.5 3.0 %exponential_reduce_fusion = f32[16384]{0:T(1024)S(1)} fusion(f32[64,16384]{1,0:T(8,128)} %param.1, f32[16384]{0:T(1024)S(1)} %add_reduce_fusion, f32[64]{0:T(128)S(1)} %subtract_bitcast_fusion), kind=kLoop, calls=%fused_computation | loop fusion | flops 3129344 | bytes 4325632 | tf_op jit(solution)/shard_map/reduce_sum | solution.py:70
  131.6 3.7 %all-to-all-done.7 = f32[4,1,16384]{2,1,0:T(1,128)S(1)} async-done(((f32[4,1,16384]{2,1,0:T(1,128)}), f32[4,1,16384]{2,1,0:T(1,128)S(1)}, u32[]{:S(2)}, u32[]{:S(2)}) %all-to-all-start.7) | async-done | bytes 262176 | tf_op jit(solution)/shard_map/all_to_all | solution.py:11
  135.3 0.8 broadcast_in_dim.46
  136.1 3.4 %all-to-all-start.8 = ((f32[4,1,16384]{2,1,0:T(1,128)}), f32[4,1,16384]{2,1,0:T(1,128)S(1)}, u32[]{:S(2)}, u32[]{:S(2)}) async-start(f32[4,1,16384]{2,1,0:T(1,128)} %broadcast_in_dim.46), calls=%async_computation.8 | async-start | bytes 524288 | tf_op jit(solution)/shard_map/all_to_all | solution.py:11
  139.5 0.2 copy.31
  139.7 1.0 slice.425
  140.7 1.0 slice.424
  141.7 4.4 %all-to-all-done.8 = f32[4,1,16384]{2,1,0:T(1,128)S(1)} async-done(((f32[4,1,16384]{2,1,0:T(1,128)}), f32[4,1,16384]{2,1,0:T(1,128)S(1)}, u32[]{:S(2)}, u32[]{:S(2)}) %all-to-all-start.8) | async-done | bytes 262176 | tf_op jit(solution)/shard_map/all_to_all | solution.py:11
  146.2 0.2 copy.30
  146.3 1.0 slice.429
  147.4 1.0 slice.428
  148.4 0.2 multiply_add_fusion
  148.6 0.9 add_negate_fusion
  (96 shorter events, 2.0 us)
Async XLA Ops:
  32.2 11.0 %all-to-all-start.1 = ((f32[4,1,16384]{2,1,0:T(1,128)}), f32[4,1,16384]{2,1,0:T(1,128)S(1)}, u32[]{:S(2)}, u32[]{:S(2)}) async-start(f32[4,1,16384]{2,1,0:T(1,128)} %broadcast_in_dim.19), calls=%async_computation.1 | async-start | bytes 524288 | tf_op jit(solution)/shard_map/all_to_all | solution.py:11
  44.0 10.1 %all-to-all-start.2 = ((f32[4,1,16384]{2,1,0:T(1,128)}), f32[4,1,16384]{2,1,0:T(1,128)S(1)}, u32[]{:S(2)}, u32[]{:S(2)}) async-start(f32[4,1,16384]{2,1,0:T(1,128)} %broadcast_in_dim.40), calls=%async_computation.2 | async-start | bytes 524288 | tf_op jit(solution)/shard_map/all_to_all | solution.py:11
  56.2 3.5 %copy-start = (f32[64,16384]{1,0:T(8,128)S(1)}, f32[64,16384]{1,0:T(8,128)}, u32[]{:S(2)}) copy-start(f32[64,16384]{1,0:T(8,128)} %param.1) | copy-start | bytes 12582916
  79.1 10.2 %all-to-all-start.4 = ((f32[4,1,16384]{2,1,0:T(1,128)}), f32[4,1,16384]{2,1,0:T(1,128)S(1)}, u32[]{:S(2)}, u32[]{:S(2)}) async-start(f32[4,1,16384]{2,1,0:T(1,128)} %broadcast_in_dim.42), calls=%async_computation.4 | async-start | bytes 524288 | tf_op jit(solution)/shard_map/all_to_all | solution.py:11
  90.0 10.1 %all-to-all-start.5 = ((f32[4,1,16384]{2,1,0:T(1,128)}), f32[4,1,16384]{2,1,0:T(1,128)S(1)}, u32[]{:S(2)}, u32[]{:S(2)}) async-start(f32[4,1,16384]{2,1,0:T(1,128)} %broadcast_in_dim.43), calls=%async_computation.5 | async-start | bytes 524288 | tf_op jit(solution)/shard_map/all_to_all | solution.py:11
  102.3 3.5 %copy-start.1 = (f32[64,16384]{1,0:T(8,128)S(1)}, f32[64,16384]{1,0:T(8,128)}, u32[]{:S(2)}) copy-start(f32[64,16384]{1,0:T(8,128)} %param.1) | copy-start | bytes 12582916
  121.6 9.9 %copy-start.2 = (f32[64]{0:T(128)}, f32[64]{0:T(128)S(1)}, u32[]{:S(2)}) copy-start(f32[64]{0:T(128)S(1)} %subtract_bitcast_fusion) | copy-start | bytes 772
  125.1 10.2 %all-to-all-start.7 = ((f32[4,1,16384]{2,1,0:T(1,128)}), f32[4,1,16384]{2,1,0:T(1,128)S(1)}, u32[]{:S(2)}, u32[]{:S(2)}) async-start(f32[4,1,16384]{2,1,0:T(1,128)} %broadcast_in_dim.45), calls=%async_computation.7 | async-start | bytes 524288 | tf_op jit(solution)/shard_map/all_to_all | solution.py:11
  136.1 10.1 %all-to-all-start.8 = ((f32[4,1,16384]{2,1,0:T(1,128)}), f32[4,1,16384]{2,1,0:T(1,128)S(1)}, u32[]{:S(2)}, u32[]{:S(2)}) async-start(f32[4,1,16384]{2,1,0:T(1,128)} %broadcast_in_dim.46), calls=%async_computation.8 | async-start | bytes 524288 | tf_op jit(solution)/shard_map/all_to_all | solution.py:11
where the time goes:
time: 151 us; the launch traced here: 150 us
  blocking collectives  47.5 us (31%)
  other arithmetic  34.7 us (23%)
  waiting for transfers between devices  24.2 us (16%)
  starting transfers between devices  21.5 us (14%)
  local copies, waits for them, and re-layouts  20.6 us (14%)
    all_to_all x3, blocking collectives, from_everyone(): return lax.all_to_all(copies, axis, split_axis=0, concat_axis=0, tiled=True)  47.5 us
    all_to_all x6, waiting for transfers between devices, from_everyone(): return lax.all_to_all(copies, axis, split_axis=0, concat_axis=0, tiled=True)  24.2 us
    all_to_all x6, starting transfers between devices, from_everyone(): return lax.all_to_all(copies, axis, split_axis=0, concat_axis=0, tiled=True)  21.5 us
    slice x72, local copies, waits for them, and re-layouts, folded_in_pairs(): part[side::2]  13.1 us
    reduce_sum x3, other arithmetic, per_device(): local_summed = jnp.sum(jnp.exp(raised - peak[None, :]), axis=0)  9.12 us
    reduce_max x3, other arithmetic, per_device(): top = jnp.max(shifted, axis=1)  8.2 us
    reduce_max x3, other arithmetic, per_device(): peak = jnp.max(raised, axis=0)  7.96 us
    broadcast_in_dim x9, local copies, waits for them, and re-layouts, from_everyone(): copies = jnp.broadcast_to(array, (lax.axis_size(axis), *array.shape))  5.03 us
  transfers between devices with their start and end apart: 6, of which 6 were waited for; matrix products, arithmetic and copies ran while one was open for 10% of the time, Pallas kernels for 0%

commit v1 on v0

v1 whole, which is shorter than its diff:
```python
import functools

import numpy as np

import jax
import jax.numpy as jnp
from jax import lax
from jax.experimental import pallas as pl
from jax.experimental.pallas import tpu as pltpu
from jax.sharding import PartitionSpec as P

ITERS = 3
LANES = 128
CHUNKS = 8
UNROLL = 8
VMEM = pl.BlockSpec(memory_space=pltpu.VMEM)
HBM = pl.BlockSpec(memory_space=pltpu.HBM)


def lane_block(j):
    return pl.ds(pl.multiple_of(j * LANES, LANES), LANES)


def rows_to_lanes(values, experts):
    below = jnp.zeros((LANES - experts, LANES), jnp.float32)
    square = jnp.concatenate([values, below], axis=0)
    return jnp.sum(square.T, axis=0, keepdims=True)


def lanes_to_rows(row, experts):
    return jnp.broadcast_to(row, (LANES, LANES)).T[:experts]


def row_lse_kernel(x_hbm, x_ref, msg_ref, sems):
    experts, tokens = x_ref.shape
    width = tokens // CHUNKS
    copies = [
        pltpu.make_async_copy(
            x_hbm.at[:, pl.ds(i * width, width)],
            x_ref.at[:, pl.ds(i * width, width)],
            sems.at[i],
        )
        for i in range(CHUNKS)
    ]
    for copy in copies:
        copy.start()
    top = jnp.full((experts, LANES), -jnp.inf, jnp.float32)
    total = jnp.zeros((experts, LANES), jnp.float32)
    for i, copy in enumerate(copies):
        copy.wait()
        starts = range(i * width, (i + 1) * width, LANES)
        new = top
        for s in starts:
            new = jnp.maximum(new, x_ref[:, pl.ds(s, LANES)])
        if i:
            total = total * jnp.exp(top - new)
        top = new
        for s in starts:
            total = total + jnp.exp(x_ref[:, pl.ds(s, LANES)] - top)
    peak = jnp.max(top, axis=1, keepdims=True)
    summed = jnp.sum(total * jnp.exp(top - peak), axis=1, keepdims=True)
    lse = peak + jnp.log(summed)
    below = jnp.zeros((LANES - experts, LANES), jnp.float32)
    square = jnp.concatenate([jnp.broadcast_to(lse, (experts, LANES)), below], axis=0)
    msg_ref[...] = jnp.broadcast_to(square.T[:1][None], msg_ref.shape)


def column_lse_kernel(log_cap, got_ref, x_ref, e_ref, peak_ref, msg_ref, ep_ref, sum_ref):
    experts, tokens = x_ref.shape
    parts = got_ref[...]
    top = jnp.max(parts, axis=0)
    ep = log_cap - (top + jnp.log(jnp.sum(jnp.exp(parts - top[None]), axis=0)))
    ep_ref[...] = ep
    shift = lanes_to_rows(ep, experts)

    def step(k, carry):
        for n in range(UNROLL):
            j = k * UNROLL + n
            raised = x_ref[:, lane_block(j)] + shift
            peak = jnp.max(raised, axis=0, keepdims=True)
            e = jnp.exp(raised - peak)
            e_ref[:, lane_block(j)] = e
            peak_ref[pl.ds(j, 1), :] = peak
            sum_ref[pl.ds(j, 1), :] = jnp.sum(e, axis=0, keepdims=True)
        return carry

    lax.fori_loop(0, tokens // (LANES * UNROLL), step, 0)
    msg_ref[...] = jnp.broadcast_to((peak_ref[...] + jnp.log(sum_ref[...]))[None], msg_ref.shape)


def weighted_rows(e_ref, w_ref, msg_ref):
    experts, tokens = e_ref.shape

    def step(k, acc):
        for n in range(UNROLL):
            j = k * UNROLL + n
            acc = acc + e_ref[:, lane_block(j)] * w_ref[pl.ds(j, 1), :]
        return acc

    zero = jnp.zeros((experts, LANES), jnp.float32)
    acc = lax.fori_loop(0, tokens // (LANES * UNROLL), step, zero)
    msg_ref[...] = jnp.broadcast_to(rows_to_lanes(acc, experts)[None], msg_ref.shape)


def first_rows_kernel(got_ref, peak_ref, e_ref, msg_ref, f_ref, tp_ref):
    parts = got_ref[...]
    top = jnp.max(parts, axis=0)
    tp = -(top + jnp.log(jnp.sum(jnp.exp(parts - top[None]), axis=0)))
    tp_ref[...] = tp
    f_ref[...] = jnp.exp(peak_ref[...] + tp)
    weighted_rows(e_ref, f_ref, msg_ref)


def rows_kernel(got_ref, f_ref, e_ref, msg_ref, w_ref):
    w_ref[...] = f_ref[...] / jnp.sum(got_ref[...], axis=0)
    weighted_rows(e_ref, w_ref, msg_ref)


def columns_kernel(cap, log_cap, got_ref, ep1_ref, f_ref, e_ref, msg_ref, ep_ref, sum_ref):
    experts, tokens = e_ref.shape
    r = jnp.sum(got_ref[...], axis=0)
    r = jnp.where(lax.broadcasted_iota(jnp.int32, r.shape, 1) < experts, r, 1.0)
    ep_ref[...] = (ep1_ref[...] + (log_cap - jnp.log(r)))[:, :experts]
    u = lanes_to_rows(cap / r, experts)

    def step(k, carry):
        for n in range(UNROLL):
            j = k * UNROLL + n
            sum_ref[pl.ds(j, 1), :] = jnp.sum(e_ref[:, lane_block(j)] * u, axis=0, keepdims=True)
        return carry

    lax.fori_loop(0, tokens // (LANES * UNROLL), step, 0)
    msg_ref[...] = jnp.broadcast_to((f_ref[...] * sum_ref[...])[None], msg_ref.shape)


def last_kernel(got_ref, tp1_ref, tp_ref):
    tp_ref[...] = tp1_ref[...] - jnp.log(jnp.sum(got_ref[...], axis=0))


def call(kernel, shapes, args, scratch=(), specs=None, limit=24):
    return pl.pallas_call(
        kernel,
        out_shape=[jax.ShapeDtypeStruct(s, jnp.float32) for s in shapes],
        in_specs=specs or [VMEM] * len(args),
        out_specs=[VMEM] * len(shapes),
        scratch_shapes=list(scratch),
        compiler_params=pltpu.CompilerParams(vmem_limit_bytes=limit * 1024 * 1024),
    )(*args)


def exchange(array, axis):
    return lax.all_to_all(array, axis, split_axis=0, concat_axis=0, tiled=True)


def per_device(logits):
    experts, tokens = logits.shape
    token_axes, expert_axis = ("gx", "gz"), "gy"
    token_shards, expert_shards = lax.axis_size(token_axes), lax.axis_size(expert_axis)
    cap = float(tokens * token_shards) / float(experts * expert_shards)
    log_cap = float(np.log(np.float32(cap)))
    rows = tokens // LANES
    big, flat, one = (experts, tokens), (rows, LANES), (1, LANES)
    to_rows = (token_shards, 1, LANES)
    to_cols = (expert_shards, rows, LANES)
    flat_scratch = pltpu.VMEM(flat, jnp.float32)

    x, msg = call(
        row_lse_kernel, [big, to_rows], [logits],
        [pltpu.SemaphoreType.DMA((CHUNKS,))], [HBM], 49,
    )
    got = exchange(msg, token_axes)
    e, peak, msg, ep1 = call(
        functools.partial(column_lse_kernel, log_cap),
        [big, flat, to_cols, one], [got, x], [flat_scratch],
    )
    got = exchange(msg, expert_axis)
    msg, f, tp1 = call(first_rows_kernel, [to_rows, flat, flat], [got, peak, e])
    for step in range(1, ITERS):
        got = exchange(msg, token_axes)
        msg, ep = call(
            functools.partial(columns_kernel, cap, log_cap),
            [to_cols, (1, experts)], [got, ep1, f, e], [flat_scratch],
        )
        got = exchange(msg, expert_axis)
        if step < ITERS - 1:
            (msg,) = call(rows_kernel, [to_rows], [got, f, e], [flat_scratch])
    (tp,) = call(last_kernel, [flat], [got, tp1])
    return tp.reshape(tokens), ep.reshape(experts)


def solution(mesh):
    in_specs = (P("gy", ("gx", "gz")),)
    out_specs = (P(("gx", "gz")), P("gy"))
    return jax.shard_map(
        per_device, mesh=mesh, in_specs=in_specs, out_specs=out_specs, check_vma=False
    )
```

time: 151 us -> 87.1 us (0.58)
  other arithmetic: 34.7 us -> 0 us
  blocking collectives: 47.5 us -> 76.6 us
  waiting for transfers between devices: 24.2 us -> 0 us
  starting transfers between devices: 21.5 us -> 0 us
  local copies, waits for them, and re-layouts: 20.6 us -> 0 us
  Pallas kernels: 0 us -> 9.18 us
    all_to_all x3 -> x6, blocking collectives: 47.5 us -> 76.6 us  [exchange(): return lax.all_to_all(array, axis, split_axis=0, concat_axis=0, tiled=True)]
    all_to_all x6 -> x0, waiting for transfers between devices: 24.2 us -> none  [from_everyone(): return lax.all_to_all(copies, axis, split_axis=0, concat_axis=0, tiled=True)]
    all_to_all x6 -> x0, starting transfers between devices: 21.5 us -> none  [from_everyone(): return lax.all_to_all(copies, axis, split_axis=0, concat_axis=0, tiled=True)]
    reduce_max x6 -> x0, other arithmetic: 16.2 us -> none  [the longest x3 8.2 us: per_device(): top = jnp.max(shifted, axis=1)]
    reduce_sum x6 -> x0, other arithmetic: 13.9 us -> none  [the longest x3 9.12 us: per_device(): local_summed = jnp.sum(jnp.exp(raised - peak[None, :]), axis=0)]
    slice x75 -> x0, local copies, waits for them, and re-layouts: 13.3 us -> none  [the longest x72 13.1 us: folded_in_pairs(): part[side::2]]
    pallas_call x0 -> x7, Pallas kernels: none -> 9.18 us  [call(): pl.pallas_call(kernel, out_shape=[jax.ShapeDtypeStruct(s, jnp.float32) fo...]
    broadcast_in_dim x9 -> x0, local copies, waits for them, and re-layouts: 5.03 us -> none  [from_everyone(): copies = jnp.broadcast_to(array, (lax.axis_size(axis), *array.shape))]
  transfers between devices with their start and end apart: 6 -> 0, of which waited for: 6 -> 0; matrix products, arithmetic and copies ran while one was open for 10% -> 0% of each run, Pallas kernels for 0% -> 0%
where the time goes in v1:
time: 87.1 us; the launch traced here: 86.4 us
  blocking collectives  76.6 us (88%)
  Pallas kernels  9.18 us (11%)
    all_to_all x6, blocking collectives, exchange(): return lax.all_to_all(array, axis, split_axis=0, concat_axis=0, tiled=True)  76.6 us
    pallas_call x7, Pallas kernels, call(): pl.pallas_call(kernel, out_shape=[jax.ShapeDtypeStruct(s, jnp.float32) fo...  9.18 us

profile of v1, /device:TPU:8, one launch (start us, length us, event | category | flops | bytes accessed | tf_op | source)
XLA Modules:
  0.0 86.4 jit_solution(15783718944332549161)
XLA Ops:
  0.6 2.5 %shard_map.30 = (f32[64,16384]{1,0:T(8,128)S(1)}, f32[64,1,128]{2,1,0:T(1,128)S(1)}) custom-call(f32[64,16384]{1,0:T(8,128)} %x_hbm.1), custom_call_target="tpu_custom_call" | custom-call | tf_op jit(solution)/shard_map/pallas_call | solution.py:141
  3.1 20.6 %all_to_all.30.got_ref = f32[64,1,128]{2,1,0:T(1,128)S(1)} all-to-all(f32[64,1,128]{2,1,0:T(1,128)S(1)} %get-tuple-element.14), channel_id=1, replica_groups=mesh['gx'=8,'gz'=8,'gy'=4] {'gx','gz'}, dimensions={0} | all-to-all | bytes 65536 | tf_op jit(solution)/shard_map/all_to_all | solution.py:152
  23.7 1.7 %shard_map.31 = (f32[64,16384]{1,0:T(8,128)S(1)}, f32[128,128]{1,0:T(8,128)S(1)}, f32[4,128,128]{2,1,0:T(8,128)S(1)}, f32[1,128]{1,0:T(1,128)S(1)}) custom-call(f32[64,1,128]{2,1,0:T(1,128)S(1)} %all_to_all.30.got_ref, f32[64,16384]{1,0:T(8,128)S(1)} %get-tuple-element.15.x_ref), custom_call_target="tpu_custom_call" | custom-call | tf_op jit(solution)/shard_map/pallas_call | solution.py:141
  25.5 10.8 %all_to_all.31.got_ref = f32[4,128,128]{2,1,0:T(8,128)S(1)} all-to-all(f32[4,128,128]{2,1,0:T(8,128)S(1)} %get-tuple-element.16), channel_id=1, replica_groups=mesh['gx'=8,'gz'=8,'gy'=4] {'gy'}, dimensions={0} | all-to-all | bytes 524288 | tf_op jit(solution)/shard_map/all_to_all | solution.py:152
  36.2 0.8 shard_map.32
  37.1 13.4 %all_to_all.32.got_ref = f32[64,1,128]{2,1,0:T(1,128)S(1)} all-to-all(f32[64,1,128]{2,1,0:T(1,128)S(1)} %get-tuple-element.19), channel_id=1, replica_groups=mesh['gx'=8,'gz'=8,'gy'=4] {'gx','gz'}, dimensions={0} | all-to-all | bytes 65536 | tf_op jit(solution)/shard_map/all_to_all | solution.py:152
  50.5 1.4 %shard_map.33 = (f32[4,128,128]{2,1,0:T(8,128)S(1)}, f32[1,64]{1,0:T(1,128)}) custom-call(f32[64,1,128]{2,1,0:T(1,128)S(1)} %all_to_all.32.got_ref, f32[1,128]{1,0:T(1,128)S(1)} %get-tuple-element.20.ep1_ref, f32[128,128]{1,0:T(8,128)S(1)} %get-tuple-element.21.f_ref, f32[64,16384]{1,0:T(8,128)S(1)} %get-tuple-element.18.e_ref), custom_call_target="tpu_custom_call" | custom-call | tf_op jit(solution)/shard_map/pallas_call | solution.py:141
  51.9 9.2 %all_to_all.33.got_ref = f32[4,128,128]{2,1,0:T(8,128)S(1)} all-to-all(f32[4,128,128]{2,1,0:T(8,128)S(1)} %get-tuple-element.22), channel_id=1, replica_groups=mesh['gx'=8,'gz'=8,'gy'=4] {'gy'}, dimensions={0} | all-to-all | bytes 524288 | tf_op jit(solution)/shard_map/all_to_all | solution.py:152
  61.0 0.8 shard_map.34
  61.8 13.4 %all_to_all.34.got_ref = f32[64,1,128]{2,1,0:T(1,128)S(1)} all-to-all(f32[64,1,128]{2,1,0:T(1,128)S(1)} %shard_map.34), channel_id=1, replica_groups=mesh['gx'=8,'gz'=8,'gy'=4] {'gx','gz'}, dimensions={0} | all-to-all | bytes 65536 | tf_op jit(solution)/shard_map/all_to_all | solution.py:152
  75.2 1.4 %shard_map.35 = (f32[4,128,128]{2,1,0:T(8,128)S(1)}, f32[1,64]{1,0:T(1,128)}) custom-call(f32[64,1,128]{2,1,0:T(1,128)S(1)} %all_to_all.34.got_ref, f32[1,128]{1,0:T(1,128)S(1)} %get-tuple-element.20.ep1_ref, f32[128,128]{1,0:T(8,128)S(1)} %get-tuple-element.21.f_ref, f32[64,16384]{1,0:T(8,128)S(1)} %get-tuple-element.18.e_ref), custom_call_target="tpu_custom_call" | custom-call | tf_op jit(solution)/shard_map/pallas_call | solution.py:141
  76.6 9.2 %all_to_all.35.got_ref = f32[4,128,128]{2,1,0:T(8,128)S(1)} all-to-all(f32[4,128,128]{2,1,0:T(8,128)S(1)} %get-tuple-element.23), channel_id=1, replica_groups=mesh['gx'=8,'gz'=8,'gy'=4] {'gy'}, dimensions={0} | all-to-all | bytes 524288 | tf_op jit(solution)/shard_map/all_to_all | solution.py:152
  85.7 0.7 shard_map.36

commit v2 on v1

v2 whole, which is shorter than its diff:
```python
import functools

import numpy as np

import jax
import jax.numpy as jnp
from jax import lax
from jax.experimental import pallas as pl
from jax.experimental.pallas import tpu as pltpu
from jax.sharding import PartitionSpec as P

ITERS = 3
LANES = 128
SUB = 8
CHUNKS = 8
UNROLL = 8
VMEM = pl.BlockSpec(memory_space=pltpu.VMEM)
HBM = pl.BlockSpec(memory_space=pltpu.HBM)


def tile(ref, j):
    block = ref[:, pl.ds(pl.multiple_of(j * LANES, LANES), LANES)]
    return block.reshape(-1, SUB, LANES)


def classes(j):
    return pl.ds(pl.multiple_of(j * SUB, SUB), SUB)


def class_rows(ref, block, s):
    return ref[pl.ds(block * SUB * SUB + s, SUB, stride=SUB), :]


def rows_to_lanes(values):
    return jnp.sum(values.T, axis=0, keepdims=True)


def lanes_to_rows(row):
    square = jnp.broadcast_to(row, (LANES, row.shape[1])).T
    return square.reshape(-1, SUB, LANES)


def for_tiles(count, body, carry):
    def step(k, carry):
        for n in range(UNROLL):
            carry = body(k * UNROLL + n, carry)
        return carry

    return lax.fori_loop(0, count // UNROLL, step, carry)


def row_lse_kernel(x_hbm, x_ref, msg_ref, sems):
    experts, tokens = x_ref.shape
    width = tokens // CHUNKS
    copies = [
        pltpu.make_async_copy(
            x_hbm.at[:, pl.ds(i * width, width)],
            x_ref.at[:, pl.ds(i * width, width)],
            sems.at[i],
        )
        for i in range(CHUNKS)
    ]
    for copy in copies:
        copy.start()
    top = jnp.full((experts, LANES), -jnp.inf, jnp.float32)
    total = jnp.zeros((experts, LANES), jnp.float32)
    for i, copy in enumerate(copies):
        copy.wait()
        starts = range(i * width, (i + 1) * width, LANES)
        new = top
        for s in starts:
            new = jnp.maximum(new, x_ref[:, pl.ds(s, LANES)])
        if i:
            total = total * jnp.exp(top - new)
        top = new
        for s in starts:
            total = total + jnp.exp(x_ref[:, pl.ds(s, LANES)] - top)
    tops, totals = top.T, total.T
    peak = jnp.max(tops, axis=0, keepdims=True)
    summed = jnp.sum(totals * jnp.exp(tops - peak), axis=0, keepdims=True)
    msg_ref[...] = jnp.broadcast_to((peak + jnp.log(summed))[None], msg_ref.shape)


def column_lse_kernel(log_cap, got_ref, x_ref, e_ref, top_ref, msg_ref, ep_ref, sum_ref):
    tokens = x_ref.shape[1]
    parts = got_ref[...]
    most = jnp.max(parts, axis=0)
    ep = log_cap - (most + jnp.log(jnp.sum(jnp.exp(parts - most[None]), axis=0)))
    ep_ref[...] = ep
    shift = lanes_to_rows(ep)

    def body(j, carry):
        raised = tile(x_ref, j) + shift
        top = jnp.max(raised, axis=0)
        e = jnp.exp(raised - top[None])
        e_ref[:, pl.ds(pl.multiple_of(j * LANES, LANES), LANES)] = e.reshape(-1, LANES)
        top_ref[classes(j), :] = top
        sum_ref[classes(j), :] = jnp.sum(e, axis=0)
        return carry

    for_tiles(tokens // LANES, body, 0)
    for b in range(tokens // (LANES * SUB)):
        tops = [class_rows(top_ref, b, s) for s in range(SUB)]
        peak = functools.reduce(jnp.maximum, tops)
        total = sum(
            class_rows(sum_ref, b, s) * jnp.exp(tops[s] - peak) for s in range(SUB)
        )
        msg_ref[classes(b), :] = peak + jnp.log(total)


def joined(one, two, three, four):
    return (one + two) + (three + four)


def first_rows_kernel(own, g1, g2, g3, top_ref, e_ref, msg_ref, f_ref, tp_ref):
    experts, tokens = e_ref.shape
    parts = [ref[...] for ref in (own, g1, g2, g3)]
    peak = functools.reduce(jnp.maximum, parts)
    tp_ref[...] = -(peak + jnp.log(joined(*(jnp.exp(part - peak) for part in parts))))

    def body(j, acc):
        f = jnp.exp(top_ref[classes(j), :] + tp_ref[pl.ds(j, 1), :])
        f_ref[classes(j), :] = f
        return acc + tile(e_ref, j) * f[None]

    zero = jnp.zeros((experts // SUB, SUB, LANES), jnp.float32)
    acc = for_tiles(tokens // LANES, body, zero)
    msg_ref[...] = jnp.broadcast_to(
        rows_to_lanes(acc.reshape(experts, LANES))[None], msg_ref.shape
    )


def rows_kernel(own, g1, g2, g3, f_ref, e_ref, msg_ref, v_ref):
    experts, tokens = e_ref.shape
    v_ref[...] = 1.0 / joined(own[...], g1[...], g2[...], g3[...])

    def body(j, acc):
        w = f_ref[classes(j), :] * v_ref[pl.ds(j, 1), :]
        return acc + tile(e_ref, j) * w[None]

    zero = jnp.zeros((experts // SUB, SUB, LANES), jnp.float32)
    acc = for_tiles(tokens // LANES, body, zero)
    msg_ref[...] = jnp.broadcast_to(
        rows_to_lanes(acc.reshape(experts, LANES))[None], msg_ref.shape
    )


def columns_kernel(cap, got_ref, f_ref, e_ref, msg_ref, sum_ref):
    tokens = e_ref.shape[1]
    u = lanes_to_rows(cap / jnp.sum(got_ref[...], axis=0))

    def body(j, carry):
        sum_ref[classes(j), :] = jnp.sum(tile(e_ref, j) * u, axis=0) * f_ref[classes(j), :]
        return carry

    for_tiles(tokens // LANES, body, 0)
    for b in range(tokens // (LANES * SUB)):
        msg_ref[classes(b), :] = sum(class_rows(sum_ref, b, s) for s in range(SUB))


def last_kernel(log_cap, own, g1, g2, g3, tp1_ref, got_ref, ep1_ref, tp_ref, ep_ref):
    ep_ref[...] = ep1_ref[...] + (log_cap - jnp.log(jnp.sum(got_ref[...], axis=0)))
    tp_ref[...] = tp1_ref[...] - jnp.log(joined(own[...], g1[...], g2[...], g3[...]))


def call(kernel, shapes, args, scratch=(), specs=None, limit=24):
    return pl.pallas_call(
        kernel,
        out_shape=[jax.ShapeDtypeStruct(s, jnp.float32) for s in shapes],
        in_specs=specs or [VMEM] * len(args),
        out_specs=[VMEM] * len(shapes),
        scratch_shapes=list(scratch),
        compiler_params=pltpu.CompilerParams(vmem_limit_bytes=limit * 1024 * 1024),
    )(*args)


def over_tokens(array, axes):
    return lax.all_to_all(array, axes, split_axis=0, concat_axis=0, tiled=True)


def over_experts(array, axis):
    members = range(lax.axis_size(axis))
    return [array] + [
        lax.ppermute(array, axis, [(i, i ^ s) for i in members]) for s in members if s
    ]


def per_device(logits):
    experts, tokens = logits.shape
    token_axes, expert_axis = ("gx", "gz"), "gy"
    token_shards, expert_shards = lax.axis_size(token_axes), lax.axis_size(expert_axis)
    cap = float(tokens * token_shards) / float(experts * expert_shards)
    log_cap = float(np.log(np.float32(cap)))
    rows = tokens // LANES
    big, flat, wide, one = (experts, tokens), (rows, LANES), (rows * SUB, LANES), (1, experts)
    to_rows = (token_shards, 1, experts)

    x, msg = call(
        row_lse_kernel, [big, to_rows], [logits],
        [pltpu.SemaphoreType.DMA((CHUNKS,))], [HBM], 49,
    )
    got = over_tokens(msg, token_axes)
    e, top, msg, ep1 = call(
        functools.partial(column_lse_kernel, log_cap),
        [big, wide, flat, one], [got, x], [pltpu.VMEM(wide, jnp.float32)],
    )
    got = over_experts(msg, expert_axis)
    msg, f, tp1 = call(first_rows_kernel, [to_rows, wide, flat], [*got, top, e])
    for step in range(1, ITERS):
        row_parts = over_tokens(msg, token_axes)
        (msg,) = call(
            functools.partial(columns_kernel, cap),
            [flat], [row_parts, f, e], [pltpu.VMEM(wide, jnp.float32)],
        )
        got = over_experts(msg, expert_axis)
        if step < ITERS - 1:
            (msg,) = call(
                rows_kernel, [to_rows], [*got, f, e], [pltpu.VMEM(flat, jnp.float32)]
            )
    tp, ep = call(
        functools.partial(last_kernel, log_cap),
        [flat, one], [*got, tp1, row_parts, ep1],
    )
    return tp.reshape(tokens), ep.reshape(experts)


def solution(mesh):
    in_specs = (P("gy", ("gx", "gz")),)
    out_specs = (P(("gx", "gz")), P("gy"))
    return jax.shard_map(
        per_device, mesh=mesh, in_specs=in_specs, out_specs=out_specs, check_vma=False
    )
```

time: 87.1 us -> 80.3 us (0.922)
  blocking collectives: 76.6 us -> 47.5 us
  starting transfers between devices: 0 us -> 12.5 us
  waiting for transfers between devices: 0 us -> 11 us
  Pallas kernels: 9.18 us -> 8.14 us
    all_to_all x6 -> x3, blocking collectives: 76.6 us -> 47.5 us  [over_tokens(): return lax.all_to_all(array, axes, split_axis=0, concat_axis=0, tiled=True)]
    ppermute x0 -> x9, starting transfers between devices: none -> 12.5 us  [over_experts(): lax.ppermute(array, axis, [(i, i ^ s) for i in members])]
    ppermute x0 -> x9, waiting for transfers between devices: none -> 11 us  [over_experts(): lax.ppermute(array, axis, [(i, i ^ s) for i in members])]
    pallas_call x7, Pallas kernels: 9.18 us -> 8.14 us  [call(): pl.pallas_call(kernel, out_shape=[jax.ShapeDtypeStruct(s, jnp.float32) fo...]
  transfers between devices with their start and end apart: 0 -> 9, of which waited for: 0 -> 6; matrix products, arithmetic and copies ran while one was open for 0% -> 0% of each run, Pallas kernels for 0% -> 0%
where the time goes in v2:
time: 80.3 us; the launch traced here: 79.8 us
  blocking collectives  47.5 us (59%)
  starting transfers between devices  12.5 us (16%)
  waiting for transfers between devices  11 us (14%)
  Pallas kernels  8.14 us (10%)
    all_to_all x3, blocking collectives, over_tokens(): return lax.all_to_all(array, axes, split_axis=0, concat_axis=0, tiled=True)  47.5 us
    ppermute x9, starting transfers between devices, over_experts(): lax.ppermute(array, axis, [(i, i ^ s) for i in members])  12.5 us
    ppermute x9, waiting for transfers between devices, over_experts(): lax.ppermute(array, axis, [(i, i ^ s) for i in members])  11 us
    pallas_call x7, Pallas kernels, call(): pl.pallas_call(kernel, out_shape=[jax.ShapeDtypeStruct(s, jnp.float32) fo...  8.14 us
  transfers between devices with their start and end apart: 9, of which 6 were waited for; matrix products, arithmetic and copies ran while one was open for 0% of the time, Pallas kernels for 0%

profile of v2, /device:TPU:8, one launch (start us, length us, event | category | flops | bytes accessed | tf_op | source)
XLA Modules:
  0.0 79.8 jit_solution(7025646209917085465)
XLA Ops:
  0.6 2.4 %shard_map.30 = (f32[64,16384]{1,0:T(8,128)S(1)}, f32[64,1,64]{2,1,0:T(1,128)S(1)}) custom-call(f32[64,16384]{1,0:T(8,128)} %x_hbm.1), custom_call_target="tpu_custom_call" | custom-call | tf_op jit(solution)/shard_map/pallas_call | solution.py:167
  3.1 20.6 %all_to_all.15.got_ref = f32[64,1,64]{2,1,0:T(1,128)S(1)} all-to-all(f32[64,1,64]{2,1,0:T(1,128)S(1)} %get-tuple-element.13), channel_id=1, replica_groups=mesh['gx'=8,'gz'=8,'gy'=4] {'gx','gz'}, dimensions={0} | all-to-all | bytes 32768 | tf_op jit(solution)/shard_map/all_to_all | solution.py:178
  23.7 1.6 %shard_map.31 = (f32[64,16384]{1,0:T(8,128)S(1)}, f32[1024,128]{1,0:T(8,128)S(1)}, f32[128,128]{1,0:T(8,128)S(1)}, f32[1,64]{1,0:T(1,128)S(1)}) custom-call(f32[64,1,64]{2,1,0:T(1,128)S(1)} %all_to_all.15.got_ref, f32[64,16384]{1,0:T(8,128)S(1)} %get-tuple-element.14.x_ref), custom_call_target="tpu_custom_call" | custom-call | tf_op jit(solution)/shard_map/pallas_call | solution.py:167
  25.3 2.8 %collective-permute-start.2 = (f32[128,128]{1,0:T(8,128)S(1)}, f32[128,128]{1,0:T(8,128)S(1)}, u32[]{:S(2)}, u32[]{:S(2)}) collective-permute-start(f32[128,128]{1,0:T(8,128)S(1)} %get-tuple-element.15.own), channel_id=1, source_target_pairs={{0,3},{1,2},{2,1},{3,0},{4,7},{5,6},{6,5},{7,4},{8,11},{9,10},{10,... | collective-permute-start | bytes 196616 | tf_op jit(solution)/shard_map/ppermute | solution.py:184
  28.1 0.8 %collective-permute-start.1 = (f32[128,128]{1,0:T(8,128)S(1)}, f32[128,128]{1,0:T(8,128)S(1)}, u32[]{:S(2)}, u32[]{:S(2)}) collective-permute-start(f32[128,128]{1,0:T(8,128)S(1)} %get-tuple-element.15.own), channel_id=1, source_target_pairs={{0,2},{1,3},{2,0},{3,1},{4,6},{5,7},{6,4},{7,5},{8,10},{9,11},{10,... | collective-permute-start | bytes 196616 | tf_op jit(solution)/shard_map/ppermute | solution.py:184
  28.9 0.5 collective-permute-start
  29.5 1.4 %collective-permute-done.2.g3 = f32[128,128]{1,0:T(8,128)S(1)} collective-permute-done((f32[128,128]{1,0:T(8,128)S(1)}, f32[128,128]{1,0:T(8,128)S(1)}, u32[]{:S(2)}, u32[]{:S(2)}) %collective-permute-start.2) | collective-permute-done | bytes 65568 | tf_op jit(solution)/shard_map/ppermute | solution.py:184
  30.9 3.1 %collective-permute-done.1.g2 = f32[128,128]{1,0:T(8,128)S(1)} collective-permute-done((f32[128,128]{1,0:T(8,128)S(1)}, f32[128,128]{1,0:T(8,128)S(1)}, u32[]{:S(2)}, u32[]{:S(2)}) %collective-permute-start.1) | collective-permute-done | bytes 65568 | tf_op jit(solution)/shard_map/ppermute | solution.py:184
  33.9 0.0 collective-permute-done.g1
  33.9 0.8 %shard_map.32 = (f32[64,1,64]{2,1,0:T(1,128)S(1)}, f32[1024,128]{1,0:T(8,128)S(1)}, f32[128,128]{1,0:T(8,128)S(1)}) custom-call(f32[128,128]{1,0:T(8,128)S(1)} %get-tuple-element.15.own, f32[128,128]{1,0:T(8,128)S(1)} %collective-permute-done.g1, f32[128,128]{1,0:T(8,128)S(1)} %collective-permute-done.1.g2, f32[128,128]{1,0:T(8,128)S(1)} %collective-permute-done.2.g3, ...), custom_call_target="tpu_custom_call" | custom-call | tf_op jit(solution)/shard_map/pallas_call | solution.py:167
  34.8 13.4 %all_to_all.16.got_ref = f32[64,1,64]{2,1,0:T(1,128)S(1)} all-to-all(f32[64,1,64]{2,1,0:T(1,128)S(1)} %get-tuple-element.18), channel_id=1, replica_groups=mesh['gx'=8,'gz'=8,'gy'=4] {'gx','gz'}, dimensions={0} | all-to-all | bytes 32768 | tf_op jit(solution)/shard_map/all_to_all | solution.py:178
  48.2 0.9 %shard_map.33.own = f32[128,128]{1,0:T(8,128)S(1)} custom-call(f32[64,1,64]{2,1,0:T(1,128)S(1)} %all_to_all.16.got_ref, f32[1024,128]{1,0:T(8,128)S(1)} %get-tuple-element.19.f_ref, f32[64,16384]{1,0:T(8,128)S(1)} %get-tuple-element.17.e_ref), custom_call_target="tpu_custom_call" | custom-call | tf_op jit(solution)/shard_map/pallas_call | solution.py:167
  49.1 1.5 %collective-permute-start.5 = (f32[128,128]{1,0:T(8,128)S(1)}, f32[128,128]{1,0:T(8,128)S(1)}, u32[]{:S(2)}, u32[]{:S(2)}) collective-permute-start(f32[128,128]{1,0:T(8,128)S(1)} %shard_map.33.own), channel_id=1, source_target_pairs={{0,3},{1,2},{2,1},{3,0},{4,7},{5,6},{6,5},{7,4},{8,11},{9,10},{10,... | collective-permute-start | bytes 196616 | tf_op jit(solution)/shard_map/ppermute | solution.py:184
  50.6 0.9 %collective-permute-start.4 = (f32[128,128]{1,0:T(8,128)S(1)}, f32[128,128]{1,0:T(8,128)S(1)}, u32[]{:S(2)}, u32[]{:S(2)}) collective-permute-start(f32[128,128]{1,0:T(8,128)S(1)} %shard_map.33.own), channel_id=1, source_target_pairs={{0,2},{1,3},{2,0},{3,1},{4,6},{5,7},{6,4},{7,5},{8,10},{9,11},{10,... | collective-permute-start | bytes 196616 | tf_op jit(solution)/shard_map/ppermute | solution.py:184
  51.5 1.8 %collective-permute-start.3 = (f32[128,128]{1,0:T(8,128)S(1)}, f32[128,128]{1,0:T(8,128)S(1)}, u32[]{:S(2)}, u32[]{:S(2)}) collective-permute-start(f32[128,128]{1,0:T(8,128)S(1)} %shard_map.33.own), channel_id=1, source_target_pairs={{0,1},{1,0},{2,3},{3,2},{4,5},{5,4},{6,7},{7,6},{8,9},{9,8},{10,11... | collective-permute-start | bytes 196616 | tf_op jit(solution)/shard_map/ppermute | solution.py:184
  53.3 2.1 %collective-permute-done.5.g3 = f32[128,128]{1,0:T(8,128)S(1)} collective-permute-done((f32[128,128]{1,0:T(8,128)S(1)}, f32[128,128]{1,0:T(8,128)S(1)}, u32[]{:S(2)}, u32[]{:S(2)}) %collective-permute-start.5) | collective-permute-done | bytes 65568 | tf_op jit(solution)/shard_map/ppermute | solution.py:184
  55.4 1.0 %collective-permute-done.4.g2 = f32[128,128]{1,0:T(8,128)S(1)} collective-permute-done((f32[128,128]{1,0:T(8,128)S(1)}, f32[128,128]{1,0:T(8,128)S(1)}, u32[]{:S(2)}, u32[]{:S(2)}) %collective-permute-start.4) | collective-permute-done | bytes 65568 | tf_op jit(solution)/shard_map/ppermute | solution.py:184
  56.4 0.0 collective-permute-done.3.g1
  56.4 0.8 %shard_map.34 = f32[64,1,64]{2,1,0:T(1,128)S(1)} custom-call(f32[128,128]{1,0:T(8,128)S(1)} %shard_map.33.own, f32[128,128]{1,0:T(8,128)S(1)} %collective-permute-done.3.g1, f32[128,128]{1,0:T(8,128)S(1)} %collective-permute-done.4.g2, f32[128,128]{1,0:T(8,128)S(1)} %collective-permute-done.5.g3, f32[1024,128]{1,0:T(8,128)S(1)} %get-tuple-element.19.f_ref, ...), custom_call_target="tpu_custom_call" | custom-call | tf_op jit(solution)/shard_map/pallas_call | solution.py:167
  57.2 13.4 %all_to_all.17.got_ref = f32[64,1,64]{2,1,0:T(1,128)S(1)} all-to-all(f32[64,1,64]{2,1,0:T(1,128)S(1)} %shard_map.34), channel_id=1, replica_groups=mesh['gx'=8,'gz'=8,'gy'=4] {'gx','gz'}, dimensions={0} | all-to-all | bytes 32768 | tf_op jit(solution)/shard_map/all_to_all | solution.py:178
  70.6 0.9 %shard_map.35.own = f32[128,128]{1,0:T(8,128)S(1)} custom-call(f32[64,1,64]{2,1,0:T(1,128)S(1)} %all_to_all.17.got_ref, f32[1024,128]{1,0:T(8,128)S(1)} %get-tuple-element.19.f_ref, f32[64,16384]{1,0:T(8,128)S(1)} %get-tuple-element.17.e_ref), custom_call_target="tpu_custom_call" | custom-call | tf_op jit(solution)/shard_map/pallas_call | solution.py:167
  71.5 1.9 %collective-permute-start.8 = (f32[128,128]{1,0:T(8,128)S(1)}, f32[128,128]{1,0:T(8,128)S(1)}, u32[]{:S(2)}, u32[]{:S(2)}) collective-permute-start(f32[128,128]{1,0:T(8,128)S(1)} %shard_map.35.own), channel_id=1, source_target_pairs={{0,3},{1,2},{2,1},{3,0},{4,7},{5,6},{6,5},{7,4},{8,11},{9,10},{10,... | collective-permute-start | bytes 196616 | tf_op jit(solution)/shard_map/ppermute | solution.py:184
  73.4 1.4 %collective-permute-start.7 = (f32[128,128]{1,0:T(8,128)S(1)}, f32[128,128]{1,0:T(8,128)S(1)}, u32[]{:S(2)}, u32[]{:S(2)}) collective-permute-start(f32[128,128]{1,0:T(8,128)S(1)} %shard_map.35.own), channel_id=1, source_target_pairs={{0,2},{1,3},{2,0},{3,1},{4,6},{5,7},{6,4},{7,5},{8,10},{9,11},{10,... | collective-permute-start | bytes 196616 | tf_op jit(solution)/shard_map/ppermute | solution.py:184
  74.8 0.9 %collective-permute-start.6 = (f32[128,128]{1,0:T(8,128)S(1)}, f32[128,128]{1,0:T(8,128)S(1)}, u32[]{:S(2)}, u32[]{:S(2)}) collective-permute-start(f32[128,128]{1,0:T(8,128)S(1)} %shard_map.35.own), channel_id=1, source_target_pairs={{0,1},{1,0},{2,3},{3,2},{4,5},{5,4},{6,7},{7,6},{8,9},{9,8},{10,11... | collective-permute-start | bytes 196616 | tf_op jit(solution)/shard_map/ppermute | solution.py:184
  75.7 2.1 %collective-permute-done.8.g3 = f32[128,128]{1,0:T(8,128)S(1)} collective-permute-done((f32[128,128]{1,0:T(8,128)S(1)}, f32[128,128]{1,0:T(8,128)S(1)}, u32[]{:S(2)}, u32[]{:S(2)}) %collective-permute-start.8) | collective-permute-done | bytes 65568 | tf_op jit(solution)/shard_map/ppermute | solution.py:184
  77.8 1.4 %collective-permute-done.7.g2 = f32[128,128]{1,0:T(8,128)S(1)} collective-permute-done((f32[128,128]{1,0:T(8,128)S(1)}, f32[128,128]{1,0:T(8,128)S(1)}, u32[]{:S(2)}, u32[]{:S(2)}) %collective-permute-start.7) | collective-permute-done | bytes 65568 | tf_op jit(solution)/shard_map/ppermute | solution.py:184
  79.2 0.0 collective-permute-done.6.g1
  79.2 0.7 shard_map.36
Async XLA Ops:
  25.3 5.6 %collective-permute-start.2 = (f32[128,128]{1,0:T(8,128)S(1)}, f32[128,128]{1,0:T(8,128)S(1)}, u32[]{:S(2)}, u32[]{:S(2)}) collective-permute-start(f32[128,128]{1,0:T(8,128)S(1)} %get-tuple-element.15.own), channel_id=1, source_target_pairs={{0,3},{1,2},{2,1},{3,0},{4,7},{5,6},{6,5},{7,4},{8,11},{9,10},{10,... | collective-permute-start | bytes 196616 | tf_op jit(solution)/shard_map/ppermute | solution.py:184
  28.1 5.8 %collective-permute-start.1 = (f32[128,128]{1,0:T(8,128)S(1)}, f32[128,128]{1,0:T(8,128)S(1)}, u32[]{:S(2)}, u32[]{:S(2)}) collective-permute-start(f32[128,128]{1,0:T(8,128)S(1)} %get-tuple-element.15.own), channel_id=1, source_target_pairs={{0,2},{1,3},{2,0},{3,1},{4,6},{5,7},{6,4},{7,5},{8,10},{9,11},{10,... | collective-permute-start | bytes 196616 | tf_op jit(solution)/shard_map/ppermute | solution.py:184
  28.9 5.0 %collective-permute-start = (f32[128,128]{1,0:T(8,128)S(1)}, f32[128,128]{1,0:T(8,128)S(1)}, u32[]{:S(2)}, u32[]{:S(2)}) collective-permute-start(f32[128,128]{1,0:T(8,128)S(1)} %get-tuple-element.15.own), channel_id=1, source_target_pairs={{0,1},{1,0},{2,3},{3,2},{4,5},{5,4},{6,7},{7,6},{8,9},{9,8},{10,11... | collective-permute-start | bytes 196616 | tf_op jit(solution)/shard_map/ppermute | solution.py:184
  49.1 6.3 %collective-permute-start.5 = (f32[128,128]{1,0:T(8,128)S(1)}, f32[128,128]{1,0:T(8,128)S(1)}, u32[]{:S(2)}, u32[]{:S(2)}) collective-permute-start(f32[128,128]{1,0:T(8,128)S(1)} %shard_map.33.own), channel_id=1, source_target_pairs={{0,3},{1,2},{2,1},{3,0},{4,7},{5,6},{6,5},{7,4},{8,11},{9,10},{10,... | collective-permute-start | bytes 196616 | tf_op jit(solution)/shard_map/ppermute | solution.py:184
  50.6 5.8 %collective-permute-start.4 = (f32[128,128]{1,0:T(8,128)S(1)}, f32[128,128]{1,0:T(8,128)S(1)}, u32[]{:S(2)}, u32[]{:S(2)}) collective-permute-start(f32[128,128]{1,0:T(8,128)S(1)} %shard_map.33.own), channel_id=1, source_target_pairs={{0,2},{1,3},{2,0},{3,1},{4,6},{5,7},{6,4},{7,5},{8,10},{9,11},{10,... | collective-permute-start | bytes 196616 | tf_op jit(solution)/shard_map/ppermute | solution.py:184
  51.5 4.9 %collective-permute-start.3 = (f32[128,128]{1,0:T(8,128)S(1)}, f32[128,128]{1,0:T(8,128)S(1)}, u32[]{:S(2)}, u32[]{:S(2)}) collective-permute-start(f32[128,128]{1,0:T(8,128)S(1)} %shard_map.33.own), channel_id=1, source_target_pairs={{0,1},{1,0},{2,3},{3,2},{4,5},{5,4},{6,7},{7,6},{8,9},{9,8},{10,11... | collective-permute-start | bytes 196616 | tf_op jit(solution)/shard_map/ppermute | solution.py:184
  71.5 6.3 %collective-permute-start.8 = (f32[128,128]{1,0:T(8,128)S(1)}, f32[128,128]{1,0:T(8,128)S(1)}, u32[]{:S(2)}, u32[]{:S(2)}) collective-permute-start(f32[128,128]{1,0:T(8,128)S(1)} %shard_map.35.own), channel_id=1, source_target_pairs={{0,3},{1,2},{2,1},{3,0},{4,7},{5,6},{6,5},{7,4},{8,11},{9,10},{10,... | collective-permute-start | bytes 196616 | tf_op jit(solution)/shard_map/ppermute | solution.py:184
  73.4 5.8 %collective-permute-start.7 = (f32[128,128]{1,0:T(8,128)S(1)}, f32[128,128]{1,0:T(8,128)S(1)}, u32[]{:S(2)}, u32[]{:S(2)}) collective-permute-start(f32[128,128]{1,0:T(8,128)S(1)} %shard_map.35.own), channel_id=1, source_target_pairs={{0,2},{1,3},{2,0},{3,1},{4,6},{5,7},{6,4},{7,5},{8,10},{9,11},{10,... | collective-permute-start | bytes 196616 | tf_op jit(solution)/shard_map/ppermute | solution.py:184
  74.8 4.4 %collective-permute-start.6 = (f32[128,128]{1,0:T(8,128)S(1)}, f32[128,128]{1,0:T(8,128)S(1)}, u32[]{:S(2)}, u32[]{:S(2)}) collective-permute-start(f32[128,128]{1,0:T(8,128)S(1)} %shard_map.35.own), channel_id=1, source_target_pairs={{0,1},{1,0},{2,3},{3,2},{4,5},{5,4},{6,7},{7,6},{8,9},{9,8},{10,11... | collective-permute-start | bytes 196616 | tf_op jit(solution)/shard_map/ppermute | solution.py:184

commit v3 on v2

--- a/solution.py
+++ b/solution.py
@@ -12,8 +12,7 @@
 ITERS = 3
 LANES = 128
 SUB = 8
-CHUNKS = 8
-UNROLL = 8
+UNROLL = 128
 VMEM = pl.BlockSpec(memory_space=pltpu.VMEM)
 HBM = pl.BlockSpec(memory_space=pltpu.HBM)
 
@@ -51,31 +50,27 @@
 
 def row_lse_kernel(x_hbm, x_ref, msg_ref, sems):
     experts, tokens = x_ref.shape
-    width = tokens // CHUNKS
+    blocks = [pl.ds(g * SUB, SUB) for g in range(experts // SUB)]
     copies = [
-        pltpu.make_async_copy(
-            x_hbm.at[:, pl.ds(i * width, width)],
-            x_ref.at[:, pl.ds(i * width, width)],
-            sems.at[i],
-        )
-        for i in range(CHUNKS)
+        pltpu.make_async_copy(x_hbm.at[block, :], x_ref.at[block, :], sems.at[g])
+        for g, block in enumerate(blocks)
     ]
     for copy in copies:
         copy.start()
-    top = jnp.full((experts, LANES), -jnp.inf, jnp.float32)
-    total = jnp.zeros((experts, LANES), jnp.float32)
-    for i, copy in enumerate(copies):
+    tops, totals = [], []
+    for copy, block in zip(copies, blocks):
         copy.wait()
-        starts = range(i * width, (i + 1) * width, LANES)
-        new = top
-        for s in starts:
-            new = jnp.maximum(new, x_ref[:, pl.ds(s, LANES)])
-        if i:
-            total = total * jnp.exp(top - new)
-        top = new
-        for s in starts:
-            total = total + jnp.exp(x_ref[:, pl.ds(s, LANES)] - top)
-    tops, totals = top.T, total.T
+        starts = range(0, tokens, LANES)
+        tree = [x_ref[block, pl.ds(s, LANES)] for s in starts]
+        while len(tree) > 1:
+            tree = [jnp.maximum(*pair) for pair in zip(tree[::2], tree[1::2])]
+        top = tree[0]
+        parts = [jnp.zeros((SUB, LANES), jnp.float32)] * 4
+        for n, s in enumerate(starts):
+            parts[n % 4] = parts[n % 4] + jnp.exp(x_ref[block, pl.ds(s, LANES)] - top)
+        tops.append(top)
+        totals.append((parts[0] + parts[1]) + (parts[2] + parts[3]))
+    tops, totals = jnp.concatenate(tops).T, jnp.concatenate(totals).T
     peak = jnp.max(tops, axis=0, keepdims=True)
     summed = jnp.sum(totals * jnp.exp(tops - peak), axis=0, keepdims=True)
     msg_ref[...] = jnp.broadcast_to((peak + jnp.log(summed))[None], msg_ref.shape)
@@ -121,10 +116,10 @@
     def body(j, acc):
         f = jnp.exp(top_ref[classes(j), :] + tp_ref[pl.ds(j, 1), :])
         f_ref[classes(j), :] = f
-        return acc + tile(e_ref, j) * f[None]
+        return acc[1], acc[0] + tile(e_ref, j) * f[None]
 
     zero = jnp.zeros((experts // SUB, SUB, LANES), jnp.float32)
-    acc = for_tiles(tokens // LANES, body, zero)
+    acc = sum(for_tiles(tokens // LANES, body, (zero, zero)))
     msg_ref[...] = jnp.broadcast_to(
         rows_to_lanes(acc.reshape(experts, LANES))[None], msg_ref.shape
     )
@@ -136,10 +131,10 @@
 
     def body(j, acc):
         w = f_ref[classes(j), :] * v_ref[pl.ds(j, 1), :]
-        return acc + tile(e_ref, j) * w[None]
+        return acc[1], acc[0] + tile(e_ref, j) * w[None]
 
     zero = jnp.zeros((experts // SUB, SUB, LANES), jnp.float32)
-    acc = for_tiles(tokens // LANES, body, zero)
+    acc = sum(for_tiles(tokens // LANES, body, (zero, zero)))
     msg_ref[...] = jnp.broadcast_to(
         rows_to_lanes(acc.reshape(experts, LANES))[None], msg_ref.shape
     )
@@ -197,7 +192,7 @@
 
     x, msg = call(
         row_lse_kernel, [big, to_rows], [logits],
-        [pltpu.SemaphoreType.DMA((CHUNKS,))], [HBM], 49,
+        [pltpu.SemaphoreType.DMA((experts // SUB,))], [HBM], 49,
     )
     got = over_tokens(msg, token_axes)
     e, top, msg, ep1 = call(

time: 80.3 us -> 78.9 us (0.983)
  Pallas kernels: 8.14 us -> 6.7 us
    pallas_call x7, Pallas kernels: 8.14 us -> 6.7 us  [call(): pl.pallas_call(kernel, out_shape=[jax.ShapeDtypeStruct(s, jnp.float32) fo...]
where the time goes in v3:
time: 78.9 us; the launch traced here: 78.4 us
  blocking collectives  47.5 us (60%)
  starting transfers between devices  12.5 us (16%)
  waiting for transfers between devices  11 us (14%)
  Pallas kernels  6.7 us (8%)
    all_to_all x3, blocking collectives, over_tokens(): return lax.all_to_all(array, axes, split_axis=0, concat_axis=0, tiled=True)  47.5 us
    ppermute x9, starting transfers between devices, over_experts(): lax.ppermute(array, axis, [(i, i ^ s) for i in members])  12.5 us
    ppermute x9, waiting for transfers between devices, over_experts(): lax.ppermute(array, axis, [(i, i ^ s) for i in members])  11 us
    pallas_call x7, Pallas kernels, call(): pl.pallas_call(kernel, out_shape=[jax.ShapeDtypeStruct(s, jnp.float32) fo...  6.7 us
  transfers between devices with their start and end apart: 9, of which 6 were waited for; matrix products, arithmetic and copies ran while one was open for 0% of the time, Pallas kernels for 0%

profile of v3, /device:TPU:8, one launch (start us, length us, event | category | flops | bytes accessed | tf_op | source)
XLA Modules:
  0.0 78.4 jit_solution(5208025833335418999)
XLA Ops:
  0.6 2.5 %shard_map.30 = (f32[64,16384]{1,0:T(8,128)S(1)}, f32[64,1,64]{2,1,0:T(1,128)S(1)}) custom-call(f32[64,16384]{1,0:T(8,128)} %x_hbm.1), custom_call_target="tpu_custom_call" | custom-call | tf_op jit(solution)/shard_map/pallas_call | solution.py:162
  3.1 20.6 %all_to_all.15.got_ref = f32[64,1,64]{2,1,0:T(1,128)S(1)} all-to-all(f32[64,1,64]{2,1,0:T(1,128)S(1)} %get-tuple-element.13), channel_id=1, replica_groups=mesh['gx'=8,'gz'=8,'gy'=4] {'gx','gz'}, dimensions={0} | all-to-all | bytes 32768 | tf_op jit(solution)/shard_map/all_to_all | solution.py:173
  23.7 1.1 %shard_map.31 = (f32[64,16384]{1,0:T(8,128)S(1)}, f32[1024,128]{1,0:T(8,128)S(1)}, f32[128,128]{1,0:T(8,128)S(1)}, f32[1,64]{1,0:T(1,128)S(1)}) custom-call(f32[64,1,64]{2,1,0:T(1,128)S(1)} %all_to_all.15.got_ref, f32[64,16384]{1,0:T(8,128)S(1)} %get-tuple-element.14.x_ref), custom_call_target="tpu_custom_call" | custom-call | tf_op jit(solution)/shard_map/pallas_call | solution.py:162
  24.9 2.8 %collective-permute-start.2 = (f32[128,128]{1,0:T(8,128)S(1)}, f32[128,128]{1,0:T(8,128)S(1)}, u32[]{:S(2)}, u32[]{:S(2)}) collective-permute-start(f32[128,128]{1,0:T(8,128)S(1)} %get-tuple-element.15.own), channel_id=1, source_target_pairs={{0,3},{1,2},{2,1},{3,0},{4,7},{5,6},{6,5},{7,4},{8,11},{9,10},{10,... | collective-permute-start | bytes 196616 | tf_op jit(solution)/shard_map/ppermute | solution.py:179
  27.7 0.8 %collective-permute-start.1 = (f32[128,128]{1,0:T(8,128)S(1)}, f32[128,128]{1,0:T(8,128)S(1)}, u32[]{:S(2)}, u32[]{:S(2)}) collective-permute-start(f32[128,128]{1,0:T(8,128)S(1)} %get-tuple-element.15.own), channel_id=1, source_target_pairs={{0,2},{1,3},{2,0},{3,1},{4,6},{5,7},{6,4},{7,5},{8,10},{9,11},{10,... | collective-permute-start | bytes 196616 | tf_op jit(solution)/shard_map/ppermute | solution.py:179
  28.5 0.5 collective-permute-start
  29.0 1.4 %collective-permute-done.2.g3 = f32[128,128]{1,0:T(8,128)S(1)} collective-permute-done((f32[128,128]{1,0:T(8,128)S(1)}, f32[128,128]{1,0:T(8,128)S(1)}, u32[]{:S(2)}, u32[]{:S(2)}) %collective-permute-start.2) | collective-permute-done | bytes 65568 | tf_op jit(solution)/shard_map/ppermute | solution.py:179
  30.4 3.1 %collective-permute-done.1.g2 = f32[128,128]{1,0:T(8,128)S(1)} collective-permute-done((f32[128,128]{1,0:T(8,128)S(1)}, f32[128,128]{1,0:T(8,128)S(1)}, u32[]{:S(2)}, u32[]{:S(2)}) %collective-permute-start.1) | collective-permute-done | bytes 65568 | tf_op jit(solution)/shard_map/ppermute | solution.py:179
  33.5 0.0 collective-permute-done.g1
  33.5 0.7 shard_map.32
  34.2 13.4 %all_to_all.16.got_ref = f32[64,1,64]{2,1,0:T(1,128)S(1)} all-to-all(f32[64,1,64]{2,1,0:T(1,128)S(1)} %get-tuple-element.18), channel_id=1, replica_groups=mesh['gx'=8,'gz'=8,'gy'=4] {'gx','gz'}, dimensions={0} | all-to-all | bytes 32768 | tf_op jit(solution)/shard_map/all_to_all | solution.py:173
  47.6 0.5 shard_map.33.own
  48.1 1.5 %collective-permute-start.5 = (f32[128,128]{1,0:T(8,128)S(1)}, f32[128,128]{1,0:T(8,128)S(1)}, u32[]{:S(2)}, u32[]{:S(2)}) collective-permute-start(f32[128,128]{1,0:T(8,128)S(1)} %shard_map.33.own), channel_id=1, source_target_pairs={{0,3},{1,2},{2,1},{3,0},{4,7},{5,6},{6,5},{7,4},{8,11},{9,10},{10,... | collective-permute-start | bytes 196616 | tf_op jit(solution)/shard_map/ppermute | solution.py:179
  49.6 0.9 %collective-permute-start.4 = (f32[128,128]{1,0:T(8,128)S(1)}, f32[128,128]{1,0:T(8,128)S(1)}, u32[]{:S(2)}, u32[]{:S(2)}) collective-permute-start(f32[128,128]{1,0:T(8,128)S(1)} %shard_map.33.own), channel_id=1, source_target_pairs={{0,2},{1,3},{2,0},{3,1},{4,6},{5,7},{6,4},{7,5},{8,10},{9,11},{10,... | collective-permute-start | bytes 196616 | tf_op jit(solution)/shard_map/ppermute | solution.py:179
  50.6 1.8 %collective-permute-start.3 = (f32[128,128]{1,0:T(8,128)S(1)}, f32[128,128]{1,0:T(8,128)S(1)}, u32[]{:S(2)}, u32[]{:S(2)}) collective-permute-start(f32[128,128]{1,0:T(8,128)S(1)} %shard_map.33.own), channel_id=1, source_target_pairs={{0,1},{1,0},{2,3},{3,2},{4,5},{5,4},{6,7},{7,6},{8,9},{9,8},{10,11... | collective-permute-start | bytes 196616 | tf_op jit(solution)/shard_map/ppermute | solution.py:179
  52.3 2.1 %collective-permute-done.5.g3 = f32[128,128]{1,0:T(8,128)S(1)} collective-permute-done((f32[128,128]{1,0:T(8,128)S(1)}, f32[128,128]{1,0:T(8,128)S(1)}, u32[]{:S(2)}, u32[]{:S(2)}) %collective-permute-start.5) | collective-permute-done | bytes 65568 | tf_op jit(solution)/shard_map/ppermute | solution.py:179
  54.4 1.0 %collective-permute-done.4.g2 = f32[128,128]{1,0:T(8,128)S(1)} collective-permute-done((f32[128,128]{1,0:T(8,128)S(1)}, f32[128,128]{1,0:T(8,128)S(1)}, u32[]{:S(2)}, u32[]{:S(2)}) %collective-permute-start.4) | collective-permute-done | bytes 65568 | tf_op jit(solution)/shard_map/ppermute | solution.py:179
  55.4 0.0 collective-permute-done.3.g1
  55.4 0.7 shard_map.34
  56.1 13.4 %all_to_all.17.got_ref = f32[64,1,64]{2,1,0:T(1,128)S(1)} all-to-all(f32[64,1,64]{2,1,0:T(1,128)S(1)} %shard_map.34), channel_id=1, replica_groups=mesh['gx'=8,'gz'=8,'gy'=4] {'gx','gz'}, dimensions={0} | all-to-all | bytes 32768 | tf_op jit(solution)/shard_map/all_to_all | solution.py:173
  69.5 0.5 shard_map.35.own
  70.1 1.9 %collective-permute-start.8 = (f32[128,128]{1,0:T(8,128)S(1)}, f32[128,128]{1,0:T(8,128)S(1)}, u32[]{:S(2)}, u32[]{:S(2)}) collective-permute-start(f32[128,128]{1,0:T(8,128)S(1)} %shard_map.35.own), channel_id=1, source_target_pairs={{0,3},{1,2},{2,1},{3,0},{4,7},{5,6},{6,5},{7,4},{8,11},{9,10},{10,... | collective-permute-start | bytes 196616 | tf_op jit(solution)/shard_map/ppermute | solution.py:179
  72.0 1.4 %collective-permute-start.7 = (f32[128,128]{1,0:T(8,128)S(1)}, f32[128,128]{1,0:T(8,128)S(1)}, u32[]{:S(2)}, u32[]{:S(2)}) collective-permute-start(f32[128,128]{1,0:T(8,128)S(1)} %shard_map.35.own), channel_id=1, source_target_pairs={{0,2},{1,3},{2,0},{3,1},{4,6},{5,7},{6,4},{7,5},{8,10},{9,11},{10,... | collective-permute-start | bytes 196616 | tf_op jit(solution)/shard_map/ppermute | solution.py:179
  73.4 0.9 %collective-permute-start.6 = (f32[128,128]{1,0:T(8,128)S(1)}, f32[128,128]{1,0:T(8,128)S(1)}, u32[]{:S(2)}, u32[]{:S(2)}) collective-permute-start(f32[128,128]{1,0:T(8,128)S(1)} %shard_map.35.own), channel_id=1, source_target_pairs={{0,1},{1,0},{2,3},{3,2},{4,5},{5,4},{6,7},{7,6},{8,9},{9,8},{10,11... | collective-permute-start | bytes 196616 | tf_op jit(solution)/shard_map/ppermute | solution.py:179
  74.2 2.1 %collective-permute-done.8.g3 = f32[128,128]{1,0:T(8,128)S(1)} collective-permute-done((f32[128,128]{1,0:T(8,128)S(1)}, f32[128,128]{1,0:T(8,128)S(1)}, u32[]{:S(2)}, u32[]{:S(2)}) %collective-permute-start.8) | collective-permute-done | bytes 65568 | tf_op jit(solution)/shard_map/ppermute | solution.py:179
  76.3 1.4 %collective-permute-done.7.g2 = f32[128,128]{1,0:T(8,128)S(1)} collective-permute-done((f32[128,128]{1,0:T(8,128)S(1)}, f32[128,128]{1,0:T(8,128)S(1)}, u32[]{:S(2)}, u32[]{:S(2)}) %collective-permute-start.7) | collective-permute-done | bytes 65568 | tf_op jit(solution)/shard_map/ppermute | solution.py:179
  77.7 0.0 collective-permute-done.6.g1
  77.7 0.7 shard_map.36
Async XLA Ops:
  24.9 5.6 %collective-permute-start.2 = (f32[128,128]{1,0:T(8,128)S(1)}, f32[128,128]{1,0:T(8,128)S(1)}, u32[]{:S(2)}, u32[]{:S(2)}) collective-permute-start(f32[128,128]{1,0:T(8,128)S(1)} %get-tuple-element.15.own), channel_id=1, source_target_pairs={{0,3},{1,2},{2,1},{3,0},{4,7},{5,6},{6,5},{7,4},{8,11},{9,10},{10,... | collective-permute-start | bytes 196616 | tf_op jit(solution)/shard_map/ppermute | solution.py:179
  27.7 5.8 %collective-permute-start.1 = (f32[128,128]{1,0:T(8,128)S(1)}, f32[128,128]{1,0:T(8,128)S(1)}, u32[]{:S(2)}, u32[]{:S(2)}) collective-permute-start(f32[128,128]{1,0:T(8,128)S(1)} %get-tuple-element.15.own), channel_id=1, source_target_pairs={{0,2},{1,3},{2,0},{3,1},{4,6},{5,7},{6,4},{7,5},{8,10},{9,11},{10,... | collective-permute-start | bytes 196616 | tf_op jit(solution)/shard_map/ppermute | solution.py:179
  28.5 5.0 %collective-permute-start = (f32[128,128]{1,0:T(8,128)S(1)}, f32[128,128]{1,0:T(8,128)S(1)}, u32[]{:S(2)}, u32[]{:S(2)}) collective-permute-start(f32[128,128]{1,0:T(8,128)S(1)} %get-tuple-element.15.own), channel_id=1, source_target_pairs={{0,1},{1,0},{2,3},{3,2},{4,5},{5,4},{6,7},{7,6},{8,9},{9,8},{10,11... | collective-permute-start | bytes 196616 | tf_op jit(solution)/shard_map/ppermute | solution.py:179
  48.1 6.3 %collective-permute-start.5 = (f32[128,128]{1,0:T(8,128)S(1)}, f32[128,128]{1,0:T(8,128)S(1)}, u32[]{:S(2)}, u32[]{:S(2)}) collective-permute-start(f32[128,128]{1,0:T(8,128)S(1)} %shard_map.33.own), channel_id=1, source_target_pairs={{0,3},{1,2},{2,1},{3,0},{4,7},{5,6},{6,5},{7,4},{8,11},{9,10},{10,... | collective-permute-start | bytes 196616 | tf_op jit(solution)/shard_map/ppermute | solution.py:179
  49.6 5.8 %collective-permute-start.4 = (f32[128,128]{1,0:T(8,128)S(1)}, f32[128,128]{1,0:T(8,128)S(1)}, u32[]{:S(2)}, u32[]{:S(2)}) collective-permute-start(f32[128,128]{1,0:T(8,128)S(1)} %shard_map.33.own), channel_id=1, source_target_pairs={{0,2},{1,3},{2,0},{3,1},{4,6},{5,7},{6,4},{7,5},{8,10},{9,11},{10,... | collective-permute-start | bytes 196616 | tf_op jit(solution)/shard_map/ppermute | solution.py:179
  50.6 4.9 %collective-permute-start.3 = (f32[128,128]{1,0:T(8,128)S(1)}, f32[128,128]{1,0:T(8,128)S(1)}, u32[]{:S(2)}, u32[]{:S(2)}) collective-permute-start(f32[128,128]{1,0:T(8,128)S(1)} %shard_map.33.own), channel_id=1, source_target_pairs={{0,1},{1,0},{2,3},{3,2},{4,5},{5,4},{6,7},{7,6},{8,9},{9,8},{10,11... | collective-permute-start | bytes 196616 | tf_op jit(solution)/shard_map/ppermute | solution.py:179
  70.1 6.3 %collective-permute-start.8 = (f32[128,128]{1,0:T(8,128)S(1)}, f32[128,128]{1,0:T(8,128)S(1)}, u32[]{:S(2)}, u32[]{:S(2)}) collective-permute-start(f32[128,128]{1,0:T(8,128)S(1)} %shard_map.35.own), channel_id=1, source_target_pairs={{0,3},{1,2},{2,1},{3,0},{4,7},{5,6},{6,5},{7,4},{8,11},{9,10},{10,... | collective-permute-start | bytes 196616 | tf_op jit(solution)/shard_map/ppermute | solution.py:179
  72.0 5.8 %collective-permute-start.7 = (f32[128,128]{1,0:T(8,128)S(1)}, f32[128,128]{1,0:T(8,128)S(1)}, u32[]{:S(2)}, u32[]{:S(2)}) collective-permute-start(f32[128,128]{1,0:T(8,128)S(1)} %shard_map.35.own), channel_id=1, source_target_pairs={{0,2},{1,3},{2,0},{3,1},{4,6},{5,7},{6,4},{7,5},{8,10},{9,11},{10,... | collective-permute-start | bytes 196616 | tf_op jit(solution)/shard_map/ppermute | solution.py:179
  73.4 4.4 %collective-permute-start.6 = (f32[128,128]{1,0:T(8,128)S(1)}, f32[128,128]{1,0:T(8,128)S(1)}, u32[]{:S(2)}, u32[]{:S(2)}) collective-permute-start(f32[128,128]{1,0:T(8,128)S(1)} %shard_map.35.own), channel_id=1, source_target_pairs={{0,1},{1,0},{2,3},{3,2},{4,5},{5,4},{6,7},{7,6},{8,9},{9,8},{10,11... | collective-permute-start | bytes 196616 | tf_op jit(solution)/shard_map/ppermute | solution.py:179

commit v4 on v3

--- a/solution.py
+++ b/solution.py
@@ -10,6 +10,7 @@
 from jax.sharding import PartitionSpec as P
 
 ITERS = 3
+HEAD = (5, 4)
 LANES = 128
 SUB = 8
 UNROLL = 128
@@ -170,7 +171,12 @@
 
 
 def over_tokens(array, axes):
-    return lax.all_to_all(array, axes, split_axis=0, concat_axis=0, tiled=True)
+    members = list(range(lax.axis_size(axes)))
+    head = HEAD[0] * lax.axis_size(axes[1]) + HEAD[1]
+    return lax.all_to_all(
+        array, axes, split_axis=0, concat_axis=0, tiled=True,
+        axis_index_groups=[members[head:] + members[:head]],
+    )
 
 
 def over_experts(array, axis):

time: 78.9 us -> 72.5 us (0.919)
  blocking collectives: 47.5 us -> 40.9 us
    all_to_all x3, blocking collectives: 47.5 us -> 40.9 us  [over_tokens(): lax.all_to_all(array, axes, split_axis=0, concat_axis=0, tiled=True, axis...]
where the time goes in v4:
time: 72.5 us; the launch traced here: 72.3 us
  blocking collectives  40.9 us (56%)
  starting transfers between devices  12.5 us (17%)
  waiting for transfers between devices  11.4 us (16%)
  Pallas kernels  6.7 us (9%)
    all_to_all x3, blocking collectives, over_tokens(): lax.all_to_all(array, axes, split_axis=0, concat_axis=0, tiled=True, axis...  40.9 us
    ppermute x9, starting transfers between devices, over_experts(): lax.ppermute(array, axis, [(i, i ^ s) for i in members])  12.5 us
    ppermute x9, waiting for transfers between devices, over_experts(): lax.ppermute(array, axis, [(i, i ^ s) for i in members])  11.4 us
    pallas_call x7, Pallas kernels, call(): pl.pallas_call(kernel, out_shape=[jax.ShapeDtypeStruct(s, jnp.float32) fo...  6.7 us
  transfers between devices with their start and end apart: 9, of which 6 were waited for; matrix products, arithmetic and copies ran while one was open for 0% of the time, Pallas kernels for 0%

profile of v4, /device:TPU:8, one launch (start us, length us, event | category | flops | bytes accessed | tf_op | source)
XLA Modules:
  0.0 72.3 jit_solution(10236589101748123395)
XLA Ops:
  0.6 2.5 %shard_map.30 = (f32[64,16384]{1,0:T(8,128)S(1)}, f32[64,1,64]{2,1,0:T(1,128)S(1)}) custom-call(f32[64,16384]{1,0:T(8,128)} %x_hbm.1), custom_call_target="tpu_custom_call" | custom-call | tf_op jit(solution)/shard_map/pallas_call | solution.py:163
  3.1 15.9 %all_to_all.15.got_ref = f32[64,1,64]{2,1,0:T(1,128)S(1)} all-to-all(f32[64,1,64]{2,1,0:T(1,128)S(1)} %get-tuple-element.13), channel_id=1, replica_groups={{176,180,184,188,192,196,200,204,208,212,216,220,224,228,232,236,240,24..., dimensions={0} | all-to-all | bytes 32768 | tf_op jit(solution)/shard_map/all_to_all | solution.py:176
  19.0 1.1 %shard_map.31 = (f32[64,16384]{1,0:T(8,128)S(1)}, f32[1024,128]{1,0:T(8,128)S(1)}, f32[128,128]{1,0:T(8,128)S(1)}, f32[1,64]{1,0:T(1,128)S(1)}) custom-call(f32[64,1,64]{2,1,0:T(1,128)S(1)} %all_to_all.15.got_ref, f32[64,16384]{1,0:T(8,128)S(1)} %get-tuple-element.14.x_ref), custom_call_target="tpu_custom_call" | custom-call | tf_op jit(solution)/shard_map/pallas_call | solution.py:163
  20.1 2.8 %collective-permute-start.2 = (f32[128,128]{1,0:T(8,128)S(1)}, f32[128,128]{1,0:T(8,128)S(1)}, u32[]{:S(2)}, u32[]{:S(2)}) collective-permute-start(f32[128,128]{1,0:T(8,128)S(1)} %get-tuple-element.15.own), channel_id=1, source_target_pairs={{0,3},{1,2},{2,1},{3,0},{4,7},{5,6},{6,5},{7,4},{8,11},{9,10},{10,... | collective-permute-start | bytes 196616 | tf_op jit(solution)/shard_map/ppermute | solution.py:185
  23.0 0.8 %collective-permute-start.1 = (f32[128,128]{1,0:T(8,128)S(1)}, f32[128,128]{1,0:T(8,128)S(1)}, u32[]{:S(2)}, u32[]{:S(2)}) collective-permute-start(f32[128,128]{1,0:T(8,128)S(1)} %get-tuple-element.15.own), channel_id=1, source_target_pairs={{0,2},{1,3},{2,0},{3,1},{4,6},{5,7},{6,4},{7,5},{8,10},{9,11},{10,... | collective-permute-start | bytes 196616 | tf_op jit(solution)/shard_map/ppermute | solution.py:185
  23.8 0.5 collective-permute-start
  24.3 1.4 %collective-permute-done.2.g3 = f32[128,128]{1,0:T(8,128)S(1)} collective-permute-done((f32[128,128]{1,0:T(8,128)S(1)}, f32[128,128]{1,0:T(8,128)S(1)}, u32[]{:S(2)}, u32[]{:S(2)}) %collective-permute-start.2) | collective-permute-done | bytes 65568 | tf_op jit(solution)/shard_map/ppermute | solution.py:185
  25.7 3.2 %collective-permute-done.1.g2 = f32[128,128]{1,0:T(8,128)S(1)} collective-permute-done((f32[128,128]{1,0:T(8,128)S(1)}, f32[128,128]{1,0:T(8,128)S(1)}, u32[]{:S(2)}, u32[]{:S(2)}) %collective-permute-start.1) | collective-permute-done | bytes 65568 | tf_op jit(solution)/shard_map/ppermute | solution.py:185
  28.9 0.0 collective-permute-done.g1
  28.9 0.7 shard_map.32
  29.6 12.5 %all_to_all.16.got_ref = f32[64,1,64]{2,1,0:T(1,128)S(1)} all-to-all(f32[64,1,64]{2,1,0:T(1,128)S(1)} %get-tuple-element.18), channel_id=1, replica_groups={{176,180,184,188,192,196,200,204,208,212,216,220,224,228,232,236,240,24..., dimensions={0} | all-to-all | bytes 32768 | tf_op jit(solution)/shard_map/all_to_all | solution.py:176
  42.1 0.5 shard_map.33.own
  42.7 1.5 %collective-permute-start.5 = (f32[128,128]{1,0:T(8,128)S(1)}, f32[128,128]{1,0:T(8,128)S(1)}, u32[]{:S(2)}, u32[]{:S(2)}) collective-permute-start(f32[128,128]{1,0:T(8,128)S(1)} %shard_map.33.own), channel_id=1, source_target_pairs={{0,3},{1,2},{2,1},{3,0},{4,7},{5,6},{6,5},{7,4},{8,11},{9,10},{10,... | collective-permute-start | bytes 196616 | tf_op jit(solution)/shard_map/ppermute | solution.py:185
  44.1 1.1 %collective-permute-start.4 = (f32[128,128]{1,0:T(8,128)S(1)}, f32[128,128]{1,0:T(8,128)S(1)}, u32[]{:S(2)}, u32[]{:S(2)}) collective-permute-start(f32[128,128]{1,0:T(8,128)S(1)} %shard_map.33.own), channel_id=1, source_target_pairs={{0,2},{1,3},{2,0},{3,1},{4,6},{5,7},{6,4},{7,5},{8,10},{9,11},{10,... | collective-permute-start | bytes 196616 | tf_op jit(solution)/shard_map/ppermute | solution.py:185
  45.2 1.6 %collective-permute-start.3 = (f32[128,128]{1,0:T(8,128)S(1)}, f32[128,128]{1,0:T(8,128)S(1)}, u32[]{:S(2)}, u32[]{:S(2)}) collective-permute-start(f32[128,128]{1,0:T(8,128)S(1)} %shard_map.33.own), channel_id=1, source_target_pairs={{0,1},{1,0},{2,3},{3,2},{4,5},{5,4},{6,7},{7,6},{8,9},{9,8},{10,11... | collective-permute-start | bytes 196616 | tf_op jit(solution)/shard_map/ppermute | solution.py:185
  46.8 2.1 %collective-permute-done.5.g3 = f32[128,128]{1,0:T(8,128)S(1)} collective-permute-done((f32[128,128]{1,0:T(8,128)S(1)}, f32[128,128]{1,0:T(8,128)S(1)}, u32[]{:S(2)}, u32[]{:S(2)}) %collective-permute-start.5) | collective-permute-done | bytes 65568 | tf_op jit(solution)/shard_map/ppermute | solution.py:185
  48.9 1.3 %collective-permute-done.4.g2 = f32[128,128]{1,0:T(8,128)S(1)} collective-permute-done((f32[128,128]{1,0:T(8,128)S(1)}, f32[128,128]{1,0:T(8,128)S(1)}, u32[]{:S(2)}, u32[]{:S(2)}) %collective-permute-start.4) | collective-permute-done | bytes 65568 | tf_op jit(solution)/shard_map/ppermute | solution.py:185
  50.2 0.0 collective-permute-done.3.g1
  50.2 0.7 shard_map.34
  50.9 12.5 %all_to_all.17.got_ref = f32[64,1,64]{2,1,0:T(1,128)S(1)} all-to-all(f32[64,1,64]{2,1,0:T(1,128)S(1)} %shard_map.34), channel_id=1, replica_groups={{176,180,184,188,192,196,200,204,208,212,216,220,224,228,232,236,240,24..., dimensions={0} | all-to-all | bytes 32768 | tf_op jit(solution)/shard_map/all_to_all | solution.py:176
  63.4 0.5 shard_map.35.own
  63.9 1.8 %collective-permute-start.8 = (f32[128,128]{1,0:T(8,128)S(1)}, f32[128,128]{1,0:T(8,128)S(1)}, u32[]{:S(2)}, u32[]{:S(2)}) collective-permute-start(f32[128,128]{1,0:T(8,128)S(1)} %shard_map.35.own), channel_id=1, source_target_pairs={{0,3},{1,2},{2,1},{3,0},{4,7},{5,6},{6,5},{7,4},{8,11},{9,10},{10,... | collective-permute-start | bytes 196616 | tf_op jit(solution)/shard_map/ppermute | solution.py:185
  65.7 1.4 %collective-permute-start.7 = (f32[128,128]{1,0:T(8,128)S(1)}, f32[128,128]{1,0:T(8,128)S(1)}, u32[]{:S(2)}, u32[]{:S(2)}) collective-permute-start(f32[128,128]{1,0:T(8,128)S(1)} %shard_map.35.own), channel_id=1, source_target_pairs={{0,2},{1,3},{2,0},{3,1},{4,6},{5,7},{6,4},{7,5},{8,10},{9,11},{10,... | collective-permute-start | bytes 196616 | tf_op jit(solution)/shard_map/ppermute | solution.py:185
  67.1 1.0 %collective-permute-start.6 = (f32[128,128]{1,0:T(8,128)S(1)}, f32[128,128]{1,0:T(8,128)S(1)}, u32[]{:S(2)}, u32[]{:S(2)}) collective-permute-start(f32[128,128]{1,0:T(8,128)S(1)} %shard_map.35.own), channel_id=1, source_target_pairs={{0,1},{1,0},{2,3},{3,2},{4,5},{5,4},{6,7},{7,6},{8,9},{9,8},{10,11... | collective-permute-start | bytes 196616 | tf_op jit(solution)/shard_map/ppermute | solution.py:185
  68.1 1.4 %collective-permute-done.8.g3 = f32[128,128]{1,0:T(8,128)S(1)} collective-permute-done((f32[128,128]{1,0:T(8,128)S(1)}, f32[128,128]{1,0:T(8,128)S(1)}, u32[]{:S(2)}, u32[]{:S(2)}) %collective-permute-start.8) | collective-permute-done | bytes 65568 | tf_op jit(solution)/shard_map/ppermute | solution.py:185
  69.5 2.1 %collective-permute-done.7.g2 = f32[128,128]{1,0:T(8,128)S(1)} collective-permute-done((f32[128,128]{1,0:T(8,128)S(1)}, f32[128,128]{1,0:T(8,128)S(1)}, u32[]{:S(2)}, u32[]{:S(2)}) %collective-permute-start.7) | collective-permute-done | bytes 65568 | tf_op jit(solution)/shard_map/ppermute | solution.py:185
  71.6 0.0 collective-permute-done.6.g1
  71.6 0.7 shard_map.36
Async XLA Ops:
  20.1 5.6 %collective-permute-start.2 = (f32[128,128]{1,0:T(8,128)S(1)}, f32[128,128]{1,0:T(8,128)S(1)}, u32[]{:S(2)}, u32[]{:S(2)}) collective-permute-start(f32[128,128]{1,0:T(8,128)S(1)} %get-tuple-element.15.own), channel_id=1, source_target_pairs={{0,3},{1,2},{2,1},{3,0},{4,7},{5,6},{6,5},{7,4},{8,11},{9,10},{10,... | collective-permute-start | bytes 196616 | tf_op jit(solution)/shard_map/ppermute | solution.py:185
  23.0 5.9 %collective-permute-start.1 = (f32[128,128]{1,0:T(8,128)S(1)}, f32[128,128]{1,0:T(8,128)S(1)}, u32[]{:S(2)}, u32[]{:S(2)}) collective-permute-start(f32[128,128]{1,0:T(8,128)S(1)} %get-tuple-element.15.own), channel_id=1, source_target_pairs={{0,2},{1,3},{2,0},{3,1},{4,6},{5,7},{6,4},{7,5},{8,10},{9,11},{10,... | collective-permute-start | bytes 196616 | tf_op jit(solution)/shard_map/ppermute | solution.py:185
  23.8 5.1 %collective-permute-start = (f32[128,128]{1,0:T(8,128)S(1)}, f32[128,128]{1,0:T(8,128)S(1)}, u32[]{:S(2)}, u32[]{:S(2)}) collective-permute-start(f32[128,128]{1,0:T(8,128)S(1)} %get-tuple-element.15.own), channel_id=1, source_target_pairs={{0,1},{1,0},{2,3},{3,2},{4,5},{5,4},{6,7},{7,6},{8,9},{9,8},{10,11... | collective-permute-start | bytes 196616 | tf_op jit(solution)/shard_map/ppermute | solution.py:185
  42.7 6.3 %collective-permute-start.5 = (f32[128,128]{1,0:T(8,128)S(1)}, f32[128,128]{1,0:T(8,128)S(1)}, u32[]{:S(2)}, u32[]{:S(2)}) collective-permute-start(f32[128,128]{1,0:T(8,128)S(1)} %shard_map.33.own), channel_id=1, source_target_pairs={{0,3},{1,2},{2,1},{3,0},{4,7},{5,6},{6,5},{7,4},{8,11},{9,10},{10,... | collective-permute-start | bytes 196616 | tf_op jit(solution)/shard_map/ppermute | solution.py:185
  44.1 6.1 %collective-permute-start.4 = (f32[128,128]{1,0:T(8,128)S(1)}, f32[128,128]{1,0:T(8,128)S(1)}, u32[]{:S(2)}, u32[]{:S(2)}) collective-permute-start(f32[128,128]{1,0:T(8,128)S(1)} %shard_map.33.own), channel_id=1, source_target_pairs={{0,2},{1,3},{2,0},{3,1},{4,6},{5,7},{6,4},{7,5},{8,10},{9,11},{10,... | collective-permute-start | bytes 196616 | tf_op jit(solution)/shard_map/ppermute | solution.py:185
  45.2 5.0 %collective-permute-start.3 = (f32[128,128]{1,0:T(8,128)S(1)}, f32[128,128]{1,0:T(8,128)S(1)}, u32[]{:S(2)}, u32[]{:S(2)}) collective-permute-start(f32[128,128]{1,0:T(8,128)S(1)} %shard_map.33.own), channel_id=1, source_target_pairs={{0,1},{1,0},{2,3},{3,2},{4,5},{5,4},{6,7},{7,6},{8,9},{9,8},{10,11... | collective-permute-start | bytes 196616 | tf_op jit(solution)/shard_map/ppermute | solution.py:185
  63.9 5.6 %collective-permute-start.8 = (f32[128,128]{1,0:T(8,128)S(1)}, f32[128,128]{1,0:T(8,128)S(1)}, u32[]{:S(2)}, u32[]{:S(2)}) collective-permute-start(f32[128,128]{1,0:T(8,128)S(1)} %shard_map.35.own), channel_id=1, source_target_pairs={{0,3},{1,2},{2,1},{3,0},{4,7},{5,6},{6,5},{7,4},{8,11},{9,10},{10,... | collective-permute-start | bytes 196616 | tf_op jit(solution)/shard_map/ppermute | solution.py:185
  65.7 5.9 %collective-permute-start.7 = (f32[128,128]{1,0:T(8,128)S(1)}, f32[128,128]{1,0:T(8,128)S(1)}, u32[]{:S(2)}, u32[]{:S(2)}) collective-permute-start(f32[128,128]{1,0:T(8,128)S(1)} %shard_map.35.own), channel_id=1, source_target_pairs={{0,2},{1,3},{2,0},{3,1},{4,6},{5,7},{6,4},{7,5},{8,10},{9,11},{10,... | collective-permute-start | bytes 196616 | tf_op jit(solution)/shard_map/ppermute | solution.py:185
  67.1 4.5 %collective-permute-start.6 = (f32[128,128]{1,0:T(8,128)S(1)}, f32[128,128]{1,0:T(8,128)S(1)}, u32[]{:S(2)}, u32[]{:S(2)}) collective-permute-start(f32[128,128]{1,0:T(8,128)S(1)} %shard_map.35.own), channel_id=1, source_target_pairs={{0,1},{1,0},{2,3},{3,2},{4,5},{5,4},{6,7},{7,6},{8,9},{9,8},{10,11... | collective-permute-start | bytes 196616 | tf_op jit(solution)/shard_map/ppermute | solution.py:185

commit v5 on v4

v5 whole, which is shorter than its diff:
```python
import functools

import numpy as np

import jax
import jax.numpy as jnp
from jax import lax
from jax.experimental import pallas as pl
from jax.experimental.pallas import tpu as pltpu
from jax.sharding import PartitionSpec as P

ITERS = 3
HEAD = (5, 4)
LANES = 128
SUB = 8
SMALLEST = 2.0**-45
VMEM = pl.BlockSpec(memory_space=pltpu.VMEM)
HBM = pl.BlockSpec(memory_space=pltpu.HBM)


def tile(ref, j):
    block = ref[:, pl.ds(pl.multiple_of(j * LANES, LANES), LANES)]
    return block.reshape(-1, SUB, LANES)


def classes(j):
    return pl.ds(pl.multiple_of(j * SUB, SUB), SUB)


def class_rows(ref, block, s):
    return ref[pl.ds(block * SUB * SUB + s, SUB, stride=SUB), :]


def rows_to_lanes(values):
    return jnp.sum(values.T, axis=0, keepdims=True)


def lanes_to_rows(row):
    square = jnp.broadcast_to(row, (LANES, row.shape[1])).T
    return square.reshape(-1, SUB, LANES)


def row_lse_kernel(x_hbm, h_ref, top_ref, msg_ref, x_ref, sems):
    experts, tokens = h_ref.shape
    blocks = [pl.ds(g * SUB, SUB) for g in range(experts // SUB)]
    copies = [
        pltpu.make_async_copy(x_hbm.at[block, :], x_ref.at[block, :], sems.at[g])
        for g, block in enumerate(blocks)
    ]
    for copy in copies:
        copy.start()
    tops, totals = [], []
    for copy, block in zip(copies, blocks):
        copy.wait()
        starts = range(0, tokens, LANES)
        tree = [x_ref[block, pl.ds(s, LANES)] for s in starts]
        while len(tree) > 1:
            tree = [jnp.maximum(*pair) for pair in zip(tree[::2], tree[1::2])]
        top = tree[0]
        parts = [jnp.zeros((SUB, LANES), jnp.float32)] * 4
        for n, s in enumerate(starts):
            h = jnp.exp(x_ref[block, pl.ds(s, LANES)] - top)
            h_ref[block, pl.ds(s, LANES)] = h
            parts[n % 4] = parts[n % 4] + h
        tops.append(top)
        totals.append((parts[0] + parts[1]) + (parts[2] + parts[3]))
    top_ref[...] = jnp.concatenate(tops)
    tops, totals = jnp.concatenate(tops).T, jnp.concatenate(totals).T
    peak = jnp.max(tops, axis=0, keepdims=True)
    summed = jnp.sum(totals * jnp.exp(tops - peak), axis=0, keepdims=True)
    msg_ref[...] = jnp.broadcast_to((peak + jnp.log(summed))[None], msg_ref.shape)


def column_sums(e_ref, weight, sum_ref):
    tokens = e_ref.shape[1]
    for j in range(tokens // LANES):
        sum_ref[classes(j), :] = jnp.sum(tile(e_ref, j) * weight, axis=0)
    for b in range(tokens // (LANES * SUB)):
        yield b, sum(class_rows(sum_ref, b, s) for s in range(SUB))


def column_lse_kernel(
    log_cap, got_ref, top_ref, x_hbm, h_ref, e_ref, w_ref, peak_ref, msg_ref, ep_ref, sum_ref, sem
):
    del h_ref
    tokens = e_ref.shape[1]
    parts = got_ref[...]
    most = jnp.max(parts, axis=0)
    ep = log_cap - (most + jnp.log(jnp.sum(jnp.exp(parts - most[None]), axis=0)))
    ep_ref[...] = ep
    shift = lanes_to_rows(ep)
    weight = jnp.exp(top_ref[...].reshape(-1, SUB, LANES) + shift)
    w_ref[...] = weight.reshape(-1, LANES)
    peak_ref[...] = jnp.zeros_like(peak_ref)
    heaviest = jnp.max(jnp.max(weight, axis=0), axis=0, keepdims=True)
    bound = jnp.maximum(heaviest, 1.0) * SMALLEST
    short = jnp.zeros((SUB, LANES), jnp.float32)
    for b, total in column_sums(e_ref, weight, sum_ref):
        msg_ref[classes(b), :] = jnp.log(total)
        short = jnp.maximum(short, jnp.where(total >= bound, 0.0, 1.0))

    @pl.when(jnp.max(short) > 0.0)
    def _():
        copy = pltpu.make_async_copy(x_hbm, e_ref, sem)
        copy.start()
        copy.wait()
        w_ref[...] = jnp.ones_like(w_ref)

        def body(j, carry):
            raised = tile(e_ref, j) + shift
            peak = jnp.max(jnp.max(raised, axis=0), axis=0, keepdims=True)
            e = jnp.exp(raised - peak[None])
            e_ref[:, pl.ds(pl.multiple_of(j * LANES, LANES), LANES)] = e.reshape(-1, LANES)
            peak_ref[pl.ds(j, 1), :] = peak
            total = jnp.sum(jnp.sum(e, axis=0), axis=0, keepdims=True)
            msg_ref[pl.ds(j, 1), :] = peak + jnp.log(total)
            return carry

        lax.fori_loop(0, tokens // LANES, body, 0)


def joined(one, two, three, four):
    return (one + two) + (three + four)


def weighted_rows(e_ref, w_ref, v_ref, msg_ref):
    experts, tokens = e_ref.shape
    acc = [jnp.zeros((experts // SUB, SUB, LANES), jnp.float32)] * 2
    for j in range(tokens // LANES):
        acc[j % 2] = acc[j % 2] + tile(e_ref, j) * v_ref[pl.ds(j, 1), :][None]
    total = (acc[0] + acc[1]).reshape(experts, LANES) * w_ref[...]
    msg_ref[...] = jnp.broadcast_to(rows_to_lanes(total)[None], msg_ref.shape)


def first_rows_kernel(own, g1, g2, g3, peak_ref, w_ref, e_ref, msg_ref, f_ref, tp_ref):
    parts = [ref[...] for ref in (own, g1, g2, g3)]
    peak = functools.reduce(jnp.maximum, parts)
    tp = -(peak + jnp.log(joined(*(jnp.exp(part - peak) for part in parts))))
    tp_ref[...] = tp
    f_ref[...] = jnp.exp(peak_ref[...] + tp)
    weighted_rows(e_ref, w_ref, f_ref, msg_ref)


def rows_kernel(own, g1, g2, g3, f_ref, w_ref, e_ref, msg_ref, v_ref):
    v_ref[...] = f_ref[...] / joined(own[...], g1[...], g2[...], g3[...])
    weighted_rows(e_ref, w_ref, v_ref, msg_ref)


def columns_kernel(cap, got_ref, f_ref, w_ref, e_ref, msg_ref, sum_ref):
    u = lanes_to_rows(cap / jnp.sum(got_ref[...], axis=0))
    weight = u * w_ref[...].reshape(-1, SUB, LANES)
    for b, total in column_sums(e_ref, weight, sum_ref):
        msg_ref[classes(b), :] = f_ref[classes(b), :] * total


def last_kernel(log_cap, own, g1, g2, g3, tp1_ref, got_ref, ep1_ref, tp_ref, ep_ref):
    ep_ref[...] = ep1_ref[...] + (log_cap - jnp.log(jnp.sum(got_ref[...], axis=0)))
    tp_ref[...] = tp1_ref[...] - jnp.log(joined(own[...], g1[...], g2[...], g3[...]))


def call(kernel, shapes, args, scratch=(), specs=None, limit=24, aliases=None):
    return pl.pallas_call(
        kernel,
        out_shape=[jax.ShapeDtypeStruct(s, jnp.float32) for s in shapes],
        in_specs=specs or [VMEM] * len(args),
        out_specs=[VMEM] * len(shapes),
        scratch_shapes=list(scratch),
        input_output_aliases=aliases or {},
        compiler_params=pltpu.CompilerParams(vmem_limit_bytes=limit * 1024 * 1024),
    )(*args)


def over_tokens(array, axes):
    members = list(range(lax.axis_size(axes)))
    head = HEAD[0] * lax.axis_size(axes[1]) + HEAD[1]
    return lax.all_to_all(
        array, axes, split_axis=0, concat_axis=0, tiled=True,
        axis_index_groups=[members[head:] + members[:head]],
    )


def over_experts(array, axis):
    members = range(lax.axis_size(axis))
    return [array] + [
        lax.ppermute(array, axis, [(i, i ^ s) for i in members]) for s in members if s
    ]


def per_device(logits):
    experts, tokens = logits.shape
    token_axes, expert_axis = ("gx", "gz"), "gy"
    token_shards, expert_shards = lax.axis_size(token_axes), lax.axis_size(expert_axis)
    cap = float(tokens * token_shards) / float(experts * expert_shards)
    log_cap = float(np.log(np.float32(cap)))
    rows = tokens // LANES
    big, flat, wide, one = (experts, tokens), (rows, LANES), (rows * SUB, LANES), (1, experts)
    to_rows = (token_shards, 1, experts)

    lanes = (experts, LANES)
    h, top, msg = call(
        row_lse_kernel, [big, lanes, to_rows], [logits],
        [pltpu.VMEM(big, jnp.float32), pltpu.SemaphoreType.DMA((experts // SUB,))], [HBM], 49,
    )
    got = over_tokens(msg, token_axes)
    e, w, peak, msg, ep1 = call(
        functools.partial(column_lse_kernel, log_cap),
        [big, lanes, flat, flat, one], [got, top, logits, h],
        [pltpu.VMEM(wide, jnp.float32), pltpu.SemaphoreType.DMA],
        [VMEM, VMEM, HBM, VMEM], 49, {3: 0},
    )
    got = over_experts(msg, expert_axis)
    msg, f, tp1 = call(first_rows_kernel, [to_rows, flat, flat], [*got, peak, w, e])
    for step in range(1, ITERS):
        row_parts = over_tokens(msg, token_axes)
        (msg,) = call(
            functools.partial(columns_kernel, cap),
            [flat], [row_parts, f, w, e], [pltpu.VMEM(wide, jnp.float32)],
        )
        got = over_experts(msg, expert_axis)
        if step < ITERS - 1:
            (msg,) = call(
                rows_kernel, [to_rows], [*got, f, w, e], [pltpu.VMEM(flat, jnp.float32)]
            )
    tp, ep = call(
        functools.partial(last_kernel, log_cap),
        [flat, one], [*got, tp1, row_parts, ep1],
    )
    return tp.reshape(tokens), ep.reshape(experts)


def solution(mesh):
    in_specs = (P("gy", ("gx", "gz")),)
    out_specs = (P(("gx", "gz")), P("gy"))
    return jax.shard_map(
        per_device, mesh=mesh, in_specs=in_specs, out_specs=out_specs, check_vma=False
    )
```

time: 72.5 us -> 79.5 us (1.097)
  Pallas kernels: 6.7 us -> 13.7 us
    pallas_call x7, Pallas kernels: 6.7 us -> 13.7 us  [call(): pl.pallas_call(kernel, out_shape=[jax.ShapeDtypeStruct(s, jnp.float32) fo...]
where the time goes in v5:
time: 79.5 us; the launch traced here: 79.3 us
  blocking collectives  40.9 us (51%)
  Pallas kernels  13.7 us (17%)
  starting transfers between devices  12.5 us (16%)
  waiting for transfers between devices  11.4 us (14%)
    all_to_all x3, blocking collectives, over_tokens(): lax.all_to_all(array, axes, split_axis=0, concat_axis=0, tiled=True, axis...  40.9 us
    pallas_call x7, Pallas kernels, call(): pl.pallas_call(kernel, out_shape=[jax.ShapeDtypeStruct(s, jnp.float32) fo...  13.7 us
    ppermute x9, starting transfers between devices, over_experts(): lax.ppermute(array, axis, [(i, i ^ s) for i in members])  12.5 us
    ppermute x9, waiting for transfers between devices, over_experts(): lax.ppermute(array, axis, [(i, i ^ s) for i in members])  11.4 us
  transfers between devices with their start and end apart: 9, of which 6 were waited for; matrix products, arithmetic and copies ran while one was open for 0% of the time, Pallas kernels for 0%

profile of v5, /device:TPU:8, one launch (start us, length us, event | category | flops | bytes accessed | tf_op | source)
XLA Modules:
  0.0 79.3 jit_solution(12539171657666897370)
XLA Ops:
  0.6 2.5 %shard_map.30 = (f32[64,16384]{1,0:T(8,128)S(1)}, f32[64,128]{1,0:T(8,128)S(1)}, f32[64,1,64]{2,1,0:T(1,128)S(1)}) custom-call(f32[64,16384]{1,0:T(8,128)} %x_hbm.3), custom_call_target="tpu_custom_call" | custom-call | tf_op jit(solution)/shard_map/pallas_call | solution.py:162
  3.1 15.9 %all_to_all.15.got_ref = f32[64,1,64]{2,1,0:T(1,128)S(1)} all-to-all(f32[64,1,64]{2,1,0:T(1,128)S(1)} %get-tuple-element.15), channel_id=1, replica_groups={{176,180,184,188,192,196,200,204,208,212,216,220,224,228,232,236,240,24..., dimensions={0} | all-to-all | bytes 32768 | tf_op jit(solution)/shard_map/all_to_all | solution.py:176
  19.0 8.6 %shard_map.31 = (f32[64,16384]{1,0:T(8,128)S(1)}, f32[64,128]{1,0:T(8,128)S(1)}, f32[128,128]{1,0:T(8,128)S(1)}, f32[128,128]{1,0:T(8,128)S(1)}, f32[1,64]{1,0:T(1,128)S(1)}) custom-call(f32[64,1,64]{2,1,0:T(1,128)S(1)} %all_to_all.15.got_ref, f32[64,128]{1,0:T(8,128)S(1)} %get-tuple-element.16.top_ref, ...), custom_call_target="tpu_custom_call", output_to_operand_aliasing={{0}: (3, {})} | custom-call | tf_op jit(solution)/shard_map/pallas_call | solution.py:162
  27.6 2.8 %collective-permute-start.2 = (f32[128,128]{1,0:T(8,128)S(1)}, f32[128,128]{1,0:T(8,128)S(1)}, u32[]{:S(2)}, u32[]{:S(2)}) collective-permute-start(f32[128,128]{1,0:T(8,128)S(1)} %get-tuple-element.18.own), channel_id=1, source_target_pairs={{0,3},{1,2},{2,1},{3,0},{4,7},{5,6},{6,5},{7,4},{8,11},{9,10},{10,... | collective-permute-start | bytes 196616 | tf_op jit(solution)/shard_map/ppermute | solution.py:185
  30.5 0.8 %collective-permute-start.1 = (f32[128,128]{1,0:T(8,128)S(1)}, f32[128,128]{1,0:T(8,128)S(1)}, u32[]{:S(2)}, u32[]{:S(2)}) collective-permute-start(f32[128,128]{1,0:T(8,128)S(1)} %get-tuple-element.18.own), channel_id=1, source_target_pairs={{0,2},{1,3},{2,0},{3,1},{4,6},{5,7},{6,4},{7,5},{8,10},{9,11},{10,... | collective-permute-start | bytes 196616 | tf_op jit(solution)/shard_map/ppermute | solution.py:185
  31.3 0.5 collective-permute-start
  31.8 1.4 %collective-permute-done.2.g3 = f32[128,128]{1,0:T(8,128)S(1)} collective-permute-done((f32[128,128]{1,0:T(8,128)S(1)}, f32[128,128]{1,0:T(8,128)S(1)}, u32[]{:S(2)}, u32[]{:S(2)}) %collective-permute-start.2) | collective-permute-done | bytes 65568 | tf_op jit(solution)/shard_map/ppermute | solution.py:185
  33.2 3.2 %collective-permute-done.1.g2 = f32[128,128]{1,0:T(8,128)S(1)} collective-permute-done((f32[128,128]{1,0:T(8,128)S(1)}, f32[128,128]{1,0:T(8,128)S(1)}, u32[]{:S(2)}, u32[]{:S(2)}) %collective-permute-start.1) | collective-permute-done | bytes 65568 | tf_op jit(solution)/shard_map/ppermute | solution.py:185
  36.4 0.0 collective-permute-done.g1
  36.4 0.5 shard_map.32
  36.9 12.5 %all_to_all.16.got_ref = f32[64,1,64]{2,1,0:T(1,128)S(1)} all-to-all(f32[64,1,64]{2,1,0:T(1,128)S(1)} %get-tuple-element.22), channel_id=1, replica_groups={{176,180,184,188,192,196,200,204,208,212,216,220,224,228,232,236,240,24..., dimensions={0} | all-to-all | bytes 32768 | tf_op jit(solution)/shard_map/all_to_all | solution.py:176
  49.4 0.5 shard_map.33.own
  49.9 1.5 %collective-permute-start.5 = (f32[128,128]{1,0:T(8,128)S(1)}, f32[128,128]{1,0:T(8,128)S(1)}, u32[]{:S(2)}, u32[]{:S(2)}) collective-permute-start(f32[128,128]{1,0:T(8,128)S(1)} %shard_map.33.own), channel_id=1, source_target_pairs={{0,3},{1,2},{2,1},{3,0},{4,7},{5,6},{6,5},{7,4},{8,11},{9,10},{10,... | collective-permute-start | bytes 196616 | tf_op jit(solution)/shard_map/ppermute | solution.py:185
  51.4 1.1 %collective-permute-start.4 = (f32[128,128]{1,0:T(8,128)S(1)}, f32[128,128]{1,0:T(8,128)S(1)}, u32[]{:S(2)}, u32[]{:S(2)}) collective-permute-start(f32[128,128]{1,0:T(8,128)S(1)} %shard_map.33.own), channel_id=1, source_target_pairs={{0,2},{1,3},{2,0},{3,1},{4,6},{5,7},{6,4},{7,5},{8,10},{9,11},{10,... | collective-permute-start | bytes 196616 | tf_op jit(solution)/shard_map/ppermute | solution.py:185
  52.5 1.6 %collective-permute-start.3 = (f32[128,128]{1,0:T(8,128)S(1)}, f32[128,128]{1,0:T(8,128)S(1)}, u32[]{:S(2)}, u32[]{:S(2)}) collective-permute-start(f32[128,128]{1,0:T(8,128)S(1)} %shard_map.33.own), channel_id=1, source_target_pairs={{0,1},{1,0},{2,3},{3,2},{4,5},{5,4},{6,7},{7,6},{8,9},{9,8},{10,11... | collective-permute-start | bytes 196616 | tf_op jit(solution)/shard_map/ppermute | solution.py:185
  54.1 2.1 %collective-permute-done.5.g3 = f32[128,128]{1,0:T(8,128)S(1)} collective-permute-done((f32[128,128]{1,0:T(8,128)S(1)}, f32[128,128]{1,0:T(8,128)S(1)}, u32[]{:S(2)}, u32[]{:S(2)}) %collective-permute-start.5) | collective-permute-done | bytes 65568 | tf_op jit(solution)/shard_map/ppermute | solution.py:185
  56.2 1.3 %collective-permute-done.4.g2 = f32[128,128]{1,0:T(8,128)S(1)} collective-permute-done((f32[128,128]{1,0:T(8,128)S(1)}, f32[128,128]{1,0:T(8,128)S(1)}, u32[]{:S(2)}, u32[]{:S(2)}) %collective-permute-start.4) | collective-permute-done | bytes 65568 | tf_op jit(solution)/shard_map/ppermute | solution.py:185
  57.5 0.0 collective-permute-done.3.g1
  57.5 0.5 shard_map.34
  58.0 12.5 %all_to_all.17.got_ref = f32[64,1,64]{2,1,0:T(1,128)S(1)} all-to-all(f32[64,1,64]{2,1,0:T(1,128)S(1)} %shard_map.34), channel_id=1, replica_groups={{176,180,184,188,192,196,200,204,208,212,216,220,224,228,232,236,240,24..., dimensions={0} | all-to-all | bytes 32768 | tf_op jit(solution)/shard_map/all_to_all | solution.py:176
  70.5 0.5 shard_map.35.own
  71.0 1.8 %collective-permute-start.8 = (f32[128,128]{1,0:T(8,128)S(1)}, f32[128,128]{1,0:T(8,128)S(1)}, u32[]{:S(2)}, u32[]{:S(2)}) collective-permute-start(f32[128,128]{1,0:T(8,128)S(1)} %shard_map.35.own), channel_id=1, source_target_pairs={{0,3},{1,2},{2,1},{3,0},{4,7},{5,6},{6,5},{7,4},{8,11},{9,10},{10,... | collective-permute-start | bytes 196616 | tf_op jit(solution)/shard_map/ppermute | solution.py:185
  72.7 1.4 %collective-permute-start.7 = (f32[128,128]{1,0:T(8,128)S(1)}, f32[128,128]{1,0:T(8,128)S(1)}, u32[]{:S(2)}, u32[]{:S(2)}) collective-permute-start(f32[128,128]{1,0:T(8,128)S(1)} %shard_map.35.own), channel_id=1, source_target_pairs={{0,2},{1,3},{2,0},{3,1},{4,6},{5,7},{6,4},{7,5},{8,10},{9,11},{10,... | collective-permute-start | bytes 196616 | tf_op jit(solution)/shard_map/ppermute | solution.py:185
  74.1 1.0 %collective-permute-start.6 = (f32[128,128]{1,0:T(8,128)S(1)}, f32[128,128]{1,0:T(8,128)S(1)}, u32[]{:S(2)}, u32[]{:S(2)}) collective-permute-start(f32[128,128]{1,0:T(8,128)S(1)} %shard_map.35.own), channel_id=1, source_target_pairs={{0,1},{1,0},{2,3},{3,2},{4,5},{5,4},{6,7},{7,6},{8,9},{9,8},{10,11... | collective-permute-start | bytes 196616 | tf_op jit(solution)/shard_map/ppermute | solution.py:185
  75.1 1.4 %collective-permute-done.8.g3 = f32[128,128]{1,0:T(8,128)S(1)} collective-permute-done((f32[128,128]{1,0:T(8,128)S(1)}, f32[128,128]{1,0:T(8,128)S(1)}, u32[]{:S(2)}, u32[]{:S(2)}) %collective-permute-start.8) | collective-permute-done | bytes 65568 | tf_op jit(solution)/shard_map/ppermute | solution.py:185
  76.5 2.1 %collective-permute-done.7.g2 = f32[128,128]{1,0:T(8,128)S(1)} collective-permute-done((f32[128,128]{1,0:T(8,128)S(1)}, f32[128,128]{1,0:T(8,128)S(1)}, u32[]{:S(2)}, u32[]{:S(2)}) %collective-permute-start.7) | collective-permute-done | bytes 65568 | tf_op jit(solution)/shard_map/ppermute | solution.py:185
  78.6 0.0 collective-permute-done.6.g1
  78.6 0.7 shard_map.36
Async XLA Ops:
  27.6 5.6 %collective-permute-start.2 = (f32[128,128]{1,0:T(8,128)S(1)}, f32[128,128]{1,0:T(8,128)S(1)}, u32[]{:S(2)}, u32[]{:S(2)}) collective-permute-start(f32[128,128]{1,0:T(8,128)S(1)} %get-tuple-element.18.own), channel_id=1, source_target_pairs={{0,3},{1,2},{2,1},{3,0},{4,7},{5,6},{6,5},{7,4},{8,11},{9,10},{10,... | collective-permute-start | bytes 196616 | tf_op jit(solution)/shard_map/ppermute | solution.py:185
  30.5 5.9 %collective-permute-start.1 = (f32[128,128]{1,0:T(8,128)S(1)}, f32[128,128]{1,0:T(8,128)S(1)}, u32[]{:S(2)}, u32[]{:S(2)}) collective-permute-start(f32[128,128]{1,0:T(8,128)S(1)} %get-tuple-element.18.own), channel_id=1, source_target_pairs={{0,2},{1,3},{2,0},{3,1},{4,6},{5,7},{6,4},{7,5},{8,10},{9,11},{10,... | collective-permute-start | bytes 196616 | tf_op jit(solution)/shard_map/ppermute | solution.py:185
  31.3 5.1 %collective-permute-start = (f32[128,128]{1,0:T(8,128)S(1)}, f32[128,128]{1,0:T(8,128)S(1)}, u32[]{:S(2)}, u32[]{:S(2)}) collective-permute-start(f32[128,128]{1,0:T(8,128)S(1)} %get-tuple-element.18.own), channel_id=1, source_target_pairs={{0,1},{1,0},{2,3},{3,2},{4,5},{5,4},{6,7},{7,6},{8,9},{9,8},{10,11... | collective-permute-start | bytes 196616 | tf_op jit(solution)/shard_map/ppermute | solution.py:185
  49.9 6.3 %collective-permute-start.5 = (f32[128,128]{1,0:T(8,128)S(1)}, f32[128,128]{1,0:T(8,128)S(1)}, u32[]{:S(2)}, u32[]{:S(2)}) collective-permute-start(f32[128,128]{1,0:T(8,128)S(1)} %shard_map.33.own), channel_id=1, source_target_pairs={{0,3},{1,2},{2,1},{3,0},{4,7},{5,6},{6,5},{7,4},{8,11},{9,10},{10,... | collective-permute-start | bytes 196616 | tf_op jit(solution)/shard_map/ppermute | solution.py:185
  51.4 6.1 %collective-permute-start.4 = (f32[128,128]{1,0:T(8,128)S(1)}, f32[128,128]{1,0:T(8,128)S(1)}, u32[]{:S(2)}, u32[]{:S(2)}) collective-permute-start(f32[128,128]{1,0:T(8,128)S(1)} %shard_map.33.own), channel_id=1, source_target_pairs={{0,2},{1,3},{2,0},{3,1},{4,6},{5,7},{6,4},{7,5},{8,10},{9,11},{10,... | collective-permute-start | bytes 196616 | tf_op jit(solution)/shard_map/ppermute | solution.py:185
  52.5 5.0 %collective-permute-start.3 = (f32[128,128]{1,0:T(8,128)S(1)}, f32[128,128]{1,0:T(8,128)S(1)}, u32[]{:S(2)}, u32[]{:S(2)}) collective-permute-start(f32[128,128]{1,0:T(8,128)S(1)} %shard_map.33.own), channel_id=1, source_target_pairs={{0,1},{1,0},{2,3},{3,2},{4,5},{5,4},{6,7},{7,6},{8,9},{9,8},{10,11... | collective-permute-start | bytes 196616 | tf_op jit(solution)/shard_map/ppermute | solution.py:185
  71.0 5.6 %collective-permute-start.8 = (f32[128,128]{1,0:T(8,128)S(1)}, f32[128,128]{1,0:T(8,128)S(1)}, u32[]{:S(2)}, u32[]{:S(2)}) collective-permute-start(f32[128,128]{1,0:T(8,128)S(1)} %shard_map.35.own), channel_id=1, source_target_pairs={{0,3},{1,2},{2,1},{3,0},{4,7},{5,6},{6,5},{7,4},{8,11},{9,10},{10,... | collective-permute-start | bytes 196616 | tf_op jit(solution)/shard_map/ppermute | solution.py:185
  72.7 5.9 %collective-permute-start.7 = (f32[128,128]{1,0:T(8,128)S(1)}, f32[128,128]{1,0:T(8,128)S(1)}, u32[]{:S(2)}, u32[]{:S(2)}) collective-permute-start(f32[128,128]{1,0:T(8,128)S(1)} %shard_map.35.own), channel_id=1, source_target_pairs={{0,2},{1,3},{2,0},{3,1},{4,6},{5,7},{6,4},{7,5},{8,10},{9,11},{10,... | collective-permute-start | bytes 196616 | tf_op jit(solution)/shard_map/ppermute | solution.py:185
  74.1 4.5 %collective-permute-start.6 = (f32[128,128]{1,0:T(8,128)S(1)}, f32[128,128]{1,0:T(8,128)S(1)}, u32[]{:S(2)}, u32[]{:S(2)}) collective-permute-start(f32[128,128]{1,0:T(8,128)S(1)} %shard_map.35.own), channel_id=1, source_target_pairs={{0,1},{1,0},{2,3},{3,2},{4,5},{5,4},{6,7},{7,6},{8,9},{9,8},{10,11... | collective-permute-start | bytes 196616 | tf_op jit(solution)/shard_map/ppermute | solution.py:185
